TPU v7x, 128 devices: a whole 4x4x4 slice. The times are simulated.
128 devices in a mesh: pipe: 2 (over x_lo), tensor: 4 (over x_hi, core), dp: 16 (over z, y).
Axes of the slice: x: 4 (x_hi: 2, x_lo: 2; x = x_hi * 2 + x_lo), y: 4, z: 4, core: 2. Of those that a mesh axis runs over, the one named last changes fastest.
Arguments:
- inputs: bfloat16 [2, 2048, 16384], P(None, 'dp', 'tensor'), may hold values from -6 to 6
- w_in: bfloat16 [2, 16384, 1024], P('pipe', ('tensor', 'dp')), may hold values from -0.046875 to 0.046875
- w_out: bfloat16 [2, 1024, 16384], P('pipe', None, ('tensor', 'dp')), may hold values from -0.1875 to 0.1875
- cotangent: bfloat16 [2, 2048, 16384], P(None, 'dp', 'tensor'), may hold values from -6 to 6
Outputs:
- update_in: float32 [2, 16384, 1024], P('pipe', ('tensor', 'dp'))
- update_out: float32 [2, 1024, 16384], P('pipe', None, ('tensor', 'dp'))
- grad_norm: float32 [], replicated
All inputs are finite; a program needn't handle non-finite values.
Results may differ from a plain program's by a relative error of at most 0.008.
Values may be sent and summed in bfloat16 or wider, within the bound.
A program may use at most 192 MiB of HBM per device.

v0:
```python
import jax
import jax.numpy as jnp
from jax import lax
from jax.sharding import Mesh
from jax.sharding import PartitionSpec as P

CLIP_NORM = 16384
DP = ("dp_0", "dp_1")
TENSOR = ("tensor_0", "tensor_1")
PIPE_TENSOR_DP = ("pipe", "tensor_0", "tensor_1", "dp_0", "dp_1")
TENSOR_DP = ("tensor_0", "tensor_1", "dp_0", "dp_1")


def rows_first(arrays, axis, dims):
    turned = [jnp.moveaxis(a, dim, 0) for a, dim in zip(arrays, dims)]
    both = jnp.concatenate([t.reshape(len(t), -1) for t in turned], axis=1)
    filled, at, done = (lax.all_gather(both, axis, axis=0, tiled=True), 0, [])
    for t, dim in zip(turned, dims):
        section = filled[:, at : at + t[0].size].reshape(-1, *t.shape[1:])
        done.append(jnp.moveaxis(section, 0, dim))
        at += t[0].size
    return tuple(done)


def total_of_pieces(value, axis):
    return lax.all_gather(value, axis).sum(0)


def from_behind(value, axis, by):
    count = lax.axis_size(axis)
    pairs = [(i, i + by) for i in range(count) if 0 <= i + by < count]
    return lax.ppermute(value, axis, pairs)


def by_axis(value, axes):
    for axis in axes:
        value = lax.psum(value, axis)
    return value


def unit_forward(preact, unused):
    return jax.nn.silu(preact).astype(jnp.bfloat16)


def unit_backward(upward, preact):
    sigmoid_value = jax.nn.sigmoid(preact)
    return (upward * sigmoid_value * (1.0 + preact * (1.0 - sigmoid_value))).astype(jnp.bfloat16)


def kahan_add(running, carried, grad_term):
    corrected = grad_term - carried.astype(jnp.float32)
    summed = (running.astype(jnp.float32) + corrected).astype(jnp.bfloat16)
    carried = (summed.astype(jnp.float32) - running.astype(jnp.float32) - corrected).astype(
        jnp.bfloat16
    )
    return (summed, carried)


def contract_last(first_operand, second_operand):
    return lax.dot_general(
        first_operand, second_operand, (((1,), (1,)), ((), ())), preferred_element_type=jnp.float32
    )


def keep_state(state, x_part, act_part, err_part, slope_part):
    return state


def on_device(inputs, w_in, w_out, cotangent):
    sections = lax.axis_size("pipe")
    section_index = lax.axis_index("pipe")
    micro_count = inputs.shape[0]
    step_count = micro_count + sections - 1
    w_first, w_second = rows_first((w_in[0], w_out[0]), DP, (0, 1))
    section_inputs, section_seeds = (inputs, cotangent)
    groups = 1
    stat_rows = section_inputs.shape[1]

    def combine_units(partial_value, unit_fn, kept_stat):
        whole_sum = total_of_pieces(partial_value, TENSOR)
        return (whole_sum, unit_fn(whole_sum, kept_stat))

    row_count = section_inputs.shape[1]
    col_count = section_inputs.shape[2]
    hidden = w_first.shape[1]
    zero_stat = jnp.zeros((stat_rows, hidden), jnp.float32)
    zero_rows = jnp.zeros((row_count, col_count), jnp.bfloat16)
    zero_units = jnp.zeros((row_count, hidden), jnp.float32)

    def project_in(current):
        return jnp.dot(current, w_first, preferred_element_type=jnp.float32)

    def project_back(current):
        return contract_last(current, w_second)

    def no_units(current):
        return zero_units

    def residual_forward(current, activation):
        return (
            current.astype(jnp.float32)
            + jnp.dot(activation, w_second, preferred_element_type=jnp.float32)
        ).astype(jnp.bfloat16)

    def residual_backward(current, slope):
        return (current.astype(jnp.float32) + contract_last(slope, w_first)).astype(jnp.bfloat16)

    def no_rows(current, other):
        return zero_rows

    def forward_step(state_carry, step_index):
        incoming, kept_x, kept_pre, kept_act = state_carry
        micro_index = step_index - section_index
        active = jnp.logical_and(micro_index >= 0, micro_index < micro_count)
        micro_slot = jnp.clip(micro_index, 0, micro_count - 1)
        own_rows = lax.dynamic_index_in_dim(section_inputs, micro_slot, 0, False)
        current = jnp.where(section_index == 0, own_rows, incoming)
        partial_value = lax.cond(active, project_in, no_units, current)
        preact, activation = combine_units(partial_value, unit_forward, zero_stat)
        result = lax.cond(active, residual_forward, no_rows, current, activation)
        kept_x = jnp.where(
            active, lax.dynamic_update_index_in_dim(kept_x, current, micro_slot, 0), kept_x
        )
        kept_pre = jnp.where(
            active, lax.dynamic_update_index_in_dim(kept_pre, preact, micro_slot, 0), kept_pre
        )
        kept_act = jnp.where(
            active, lax.dynamic_update_index_in_dim(kept_act, activation, micro_slot, 0), kept_act
        )
        outgoing = from_behind(result, "pipe", 1)
        return ((outgoing, kept_x, kept_pre, kept_act), None)

    forward_init = (
        zero_rows,
        jnp.zeros((micro_count, row_count, col_count), jnp.bfloat16),
        jnp.zeros((micro_count, stat_rows, hidden), jnp.float32),
        jnp.zeros((micro_count, row_count, hidden), jnp.bfloat16),
    )
    forward_final, unused_out = lax.scan(forward_step, forward_init, jnp.arange(step_count))
    unused_rows, kept_x, kept_pre, kept_act = forward_final

    def accumulate(state, x_part, act_part, err_part, slope_part):
        sum_in, err_in, sum_out, err_out = state
        x_groups = x_part.reshape(groups, -1, col_count)
        slope_groups = slope_part.reshape(groups, -1, hidden)
        act_groups = act_part.reshape(groups, -1, hidden)
        err_groups = err_part.reshape(groups, -1, col_count)
        grad_in = jnp.einsum(
            "gtc,gth->gch", x_groups, slope_groups, preferred_element_type=jnp.float32
        )
        grad_out = jnp.einsum(
            "gth,gtc->ghc", act_groups, err_groups, preferred_element_type=jnp.float32
        )
        sum_in, err_in = kahan_add(sum_in, err_in, grad_in)
        sum_out, err_out = kahan_add(sum_out, err_out, grad_out)
        return (sum_in, err_in, sum_out, err_out)

    def backward_step(state_carry, step_index):
        incoming, sums = state_carry
        micro_index = step_index - (sections - 1 - section_index)
        active = jnp.logical_and(micro_index >= 0, micro_index < micro_count)
        micro_slot = jnp.clip(micro_index, 0, micro_count - 1)
        own_rows = lax.dynamic_index_in_dim(section_seeds, micro_slot, 0, False)
        current = jnp.where(section_index == sections - 1, own_rows, incoming)
        partial_value = lax.cond(active, project_back, no_units, current)
        preact = lax.dynamic_index_in_dim(kept_pre, micro_slot, 0, False)
        unused_stat, slope = combine_units(partial_value, unit_backward, preact)
        x_here = lax.dynamic_index_in_dim(kept_x, micro_slot, 0, False)
        act_here = lax.dynamic_index_in_dim(kept_act, micro_slot, 0, False)
        sums = lax.cond(active, accumulate, keep_state, sums, x_here, act_here, current, slope)
        result = lax.cond(active, residual_backward, no_rows, current, slope)
        outgoing = from_behind(result, "pipe", -1)
        return ((outgoing, sums), None)

    sums_init = (
        jnp.zeros((groups, col_count, hidden), jnp.bfloat16),
        jnp.zeros((groups, col_count, hidden), jnp.bfloat16),
        jnp.zeros((groups, hidden, col_count), jnp.bfloat16),
        jnp.zeros((groups, hidden, col_count), jnp.bfloat16),
    )
    backward_final, unused_back = lax.scan(
        backward_step, (zero_rows, sums_init), jnp.arange(step_count)
    )
    unused_errors, final_sums = backward_final
    sum_in, err_in, sum_out, err_out = final_sums
    total_in = jnp.sum(sum_in.astype(jnp.float32) - err_in.astype(jnp.float32), axis=0)
    total_out = jnp.sum(sum_out.astype(jnp.float32) - err_out.astype(jnp.float32), axis=0)
    total_in, total_out = (
        lax.psum_scatter(total_in, DP, scatter_dimension=0, tiled=True),
        lax.psum_scatter(total_out, DP, scatter_dimension=1, tiled=True),
    )
    squares = jnp.sum(total_in * total_in) + jnp.sum(total_out * total_out)
    norm_squared = by_axis(squares, PIPE_TENSOR_DP)
    grad_norm = jnp.sqrt(norm_squared)
    factor = jnp.minimum(1.0, CLIP_NORM / grad_norm)
    return ((total_in * factor)[None], (total_out * factor)[None], grad_norm)


def solution(mesh):
    split = Mesh(
        mesh.devices.reshape(mesh.shape["pipe"], 2, 2, 4, 4),
        ("pipe", "tensor_0", "tensor_1", "dp_0", "dp_1"),
    )
    placed = (
        P(None, DP, TENSOR),
        P("pipe", TENSOR_DP, None),
        P("pipe", None, TENSOR_DP),
        P(None, DP, TENSOR),
    )
    return jax.shard_map(
        on_device,
        mesh=split,
        in_specs=placed,
        out_specs=(P("pipe", TENSOR_DP, None), P("pipe", None, TENSOR_DP), P()),
        check_vma=False,
    )
```

profile of v0, /device:TPU:1, one launch (start us, length us, event | category | flops | bytes accessed | tf_op | source)
XLA Modules:
  0.0 885.3 jit_solution(17027753523874269229)
XLA Ops:
  10.6 114.5 %all-gather.10.cloned.1.call-done = bf16[4096,2048]{1,0:T(8,128)(2,1)} async-done(((bf16[256,2048]{1,0:T(8,128)(2,1)}), bf16[4096,2048]{1,0:T(8,128)(2,1)}) %all-gather.10.cloned.1.call-update) | async-done | bytes 16777232 | tf_op jit(solution)/shard_map/all_gather | solution.py:17
  125.1 11.7 %fusion.32 = (bf16[4096,1024]{1,0:T(8,128)(2,1)}, bf16[1024,4096]{0,1:T(8,128)(2,1)}) fusion(bf16[4096,2048]{1,0:T(8,128)(2,1)} %all-gather.10.cloned.1.call-done), kind=kLoop, calls=%fused_computation.55 | loop fusion | bytes 33554432 | tf_op jit(solution)/shard_map/slice | solution.py:19
  136.8 11.3 %copy.9 = bf16[1024,4096]{1,0:T(8,128)(2,1)} copy(bf16[1024,4096]{0,1:T(8,128)(2,1)} %get-tuple-element.500) | data formatting | bytes 16777216 | tf_op jit(solution)/shard_map/while | solution.py:181
  151.0 213.3 %while.37 = (s32[]{:T(128)}, bf16[128,4096]{1,0:T(8,128)(2,1)}, bf16[2,128,4096]{2,1,0:T(8,128)(2,1)}, f32[2,128,1024]{2,1,0:T(8,128)S(1)}, bf16[2,128,1024]{2,1...) while((s32[]{:T(128)}, bf16[128,4096]{1,0:T(8,128)(2,1)}, ...), condition=%wide.region_6.7_spmd, body=%wide.region_0.6_spmd.sunk | while | flops 2152071168 | bytes 50332584 | solution.py:139
  160.9 26.9 %all-gather.12.cloned.1.call-done = f32[512,1024]{1,0:T(8,128)} async-done(((f32[128,1024]{1,0:T(8,128)}), f32[512,1024]{1,0:T(8,128)}) %all-gather.12.cloned.1.call-update) | async-done | bytes 2097168 | tf_op jit(solution)/shard_map/while/body/eval_jaxpr/all_gather | solution.py:26
  197.0 22.5 %collective-permute-done = bf16[128,4096]{1,0:T(8,128)(2,1)S(1)} collective-permute-done((bf16[128,4096]{1,0:T(8,128)(2,1)}, bf16[128,4096]{1,0:T(8,128)(2,1)S(1)}, u32[]{:S(2)}, u32[]{:S(2)}) %collective-permute-start) | collective-permute-done | bytes 1048608 | tf_op jit(solution)/shard_map/while/body/eval_jaxpr/ppermute | solution.py:32
  230.3 28.3 %all-gather.12.cloned.1.call-done = f32[512,1024]{1,0:T(8,128)} async-done(((f32[128,1024]{1,0:T(8,128)}), f32[512,1024]{1,0:T(8,128)}) %all-gather.12.cloned.1.call-update) | async-done | bytes 2097168 | tf_op jit(solution)/shard_map/while/body/eval_jaxpr/all_gather | solution.py:26
  268.7 22.2 %collective-permute-done = bf16[128,4096]{1,0:T(8,128)(2,1)S(1)} collective-permute-done((bf16[128,4096]{1,0:T(8,128)(2,1)}, bf16[128,4096]{1,0:T(8,128)(2,1)S(1)}, u32[]{:S(2)}, u32[]{:S(2)}) %collective-permute-start) | collective-permute-done | bytes 1048608 | tf_op jit(solution)/shard_map/while/body/eval_jaxpr/ppermute | solution.py:32
  297.2 33.7 %all-gather.12.cloned.1.call-done = f32[512,1024]{1,0:T(8,128)} async-done(((f32[128,1024]{1,0:T(8,128)}), f32[512,1024]{1,0:T(8,128)}) %all-gather.12.cloned.1.call-update) | async-done | bytes 2097168 | tf_op jit(solution)/shard_map/while/body/eval_jaxpr/all_gather | solution.py:26
  341.1 22.2 %collective-permute-done = bf16[128,4096]{1,0:T(8,128)(2,1)S(1)} collective-permute-done((bf16[128,4096]{1,0:T(8,128)(2,1)}, bf16[128,4096]{1,0:T(8,128)(2,1)S(1)}, u32[]{:S(2)}, u32[]{:S(2)}) %collective-permute-start) | collective-permute-done | bytes 1048608 | tf_op jit(solution)/shard_map/while/body/eval_jaxpr/ppermute | solution.py:32
  381.9 219.3 %while.38 = (s32[]{:T(128)}, bf16[128,4096]{1,0:T(8,128)(2,1)S(1)}, bf16[1,4096,1024]{2,1,0:T(8,128)(2,1)}, bf16[1,4096,1024]{2,1,0:T(8,128)(2,1)}, bf16[1,1024,...) while((s32[]{:T(128)}, bf16[128,4096]{1,0:T(8,128)(2,1)S(1)}, ...), condition=%wide.region_15.16_spmd, body=%wide.region_7.15_spmd.sunk | while | flops 4374134784 | bytes 187172016 | solution.py:181
  385.6 35.1 %all-gather.14.cloned.1.call-done = f32[512,1024]{1,0:T(8,128)} async-done(((f32[128,1024]{1,0:T(8,128)}), f32[512,1024]{1,0:T(8,128)}) %all-gather.14.cloned.1.call-update) | async-done | bytes 2097168 | tf_op jit(solution)/shard_map/while/body/eval_jaxpr/all_gather | solution.py:26
  425.2 29.9 %collective-permute-done.1 = bf16[128,4096]{1,0:T(8,128)(2,1)S(1)} collective-permute-done((bf16[128,4096]{1,0:T(8,128)(2,1)}, bf16[128,4096]{1,0:T(8,128)(2,1)S(1)}, u32[]{:S(2)}, u32[]{:S(2)}) %collective-permute-start.1) | collective-permute-done | bytes 1048608 | tf_op jit(solution)/shard_map/while/body/eval_jaxpr/ppermute | solution.py:32
  464.9 28.1 %all-gather.14.cloned.1.call-done = f32[512,1024]{1,0:T(8,128)} async-done(((f32[128,1024]{1,0:T(8,128)}), f32[512,1024]{1,0:T(8,128)}) %all-gather.14.cloned.1.call-update) | async-done | bytes 2097168 | tf_op jit(solution)/shard_map/while/body/eval_jaxpr/all_gather | solution.py:26
  503.5 25.6 %conditional.14 = ((bf16[1,4096,1024]{2,1,0:T(8,128)(2,1)}, bf16[1,4096,1024]{2,1,0:T(8,128)(2,1)}, bf16[1,1024,4096]{2,1,0:T(8,128)(2,1)}, bf16[1,1024,4096]{2,1,0:T(8,128)(2,1)})) conditional(s32[]{:T(128)} %convert_element_type.173, (bf16[1,4096,1024]{2,1,0:T(8,128)(2,1)}, bf16[1,4096,1024]{2,1,0:T(8,128)(2,1)}, ...), branch_computations={%region_13.13_spmd, %region_14.14_spmd} | conditional | flops 2222981120 | bytes 136839776 | solution.py:170
  503.6 12.9 %fusion.12 = (bf16[1,4096,1024]{2,1,0:T(8,128)(2,1)}, bf16[1,4096,1024]{2,1,0:T(8,128)(2,1)}) fusion(bf16[1,4096,1024]{2,1,0:T(8,128)(2,1)} %get-tuple-element.369, bf16[1,4096,1024]{2,1,0:T(8,128)(2,1)} %get-tuple-element.373, bf16[128,1024]{1,0:T(8,128)(2,1)S(1)} %get-tuple-element.372, bf16[2,128,4096]{2,1,0:T(8,128)(2,1)} %get-tuple-element.370, ...), kind=kOutput, calls=%fused_computation.24 | convolution fusion | flops 1111490560 | bytes 34865664 | tf_op jit(solution)/shard_map/while/body/eval_jaxpr/cond/branch_1_fun/gtc,gth->gch/dot_general | solution.py:148
  516.5 9.3 %fusion.15 = (bf16[1,1024,4096]{2,1,0:T(8,128)(2,1)}, bf16[1,1024,4096]{2,1,0:T(8,128)(2,1)S(1)}) fusion(bf16[1,1024,4096]{2,1,0:T(8,128)(2,1)S(1)} %copy-done, bf16[1,1024,4096]{2,1,0:T(8,128)(2,1)} %get-tuple-element.377, bf16[128,4096]{1,0:T(8,128)(2,1)S(1)} %get-tuple-element.376, bf16[2,128,1024]{2,1,0:T(8,128)(2,1)S(1)} %get-tuple-element.375, ...), kind=kOutput, calls=%fused_computation.27 | convolution fusion | flops 1111490560 | bytes 34865156 | tf_op jit(solution)/shard_map/while/body/eval_jaxpr/cond/branch_1_fun/gth,gtc->ghc/dot_general | solution.py:151
  538.9 26.1 %all-gather.14.cloned.1.call-done = f32[512,1024]{1,0:T(8,128)} async-done(((f32[128,1024]{1,0:T(8,128)}), f32[512,1024]{1,0:T(8,128)}) %all-gather.14.cloned.1.call-update) | async-done | bytes 2097168 | tf_op jit(solution)/shard_map/while/body/eval_jaxpr/all_gather | solution.py:26
  575.6 25.6 %conditional.14 = ((bf16[1,4096,1024]{2,1,0:T(8,128)(2,1)}, bf16[1,4096,1024]{2,1,0:T(8,128)(2,1)}, bf16[1,1024,4096]{2,1,0:T(8,128)(2,1)}, bf16[1,1024,4096]{2,1,0:T(8,128)(2,1)})) conditional(s32[]{:T(128)} %convert_element_type.173, (bf16[1,4096,1024]{2,1,0:T(8,128)(2,1)}, bf16[1,4096,1024]{2,1,0:T(8,128)(2,1)}, ...), branch_computations={%region_13.13_spmd, %region_14.14_spmd} | conditional | flops 2222981120 | bytes 136839776 | solution.py:170
  575.6 12.9 %fusion.12 = (bf16[1,4096,1024]{2,1,0:T(8,128)(2,1)}, bf16[1,4096,1024]{2,1,0:T(8,128)(2,1)}) fusion(bf16[1,4096,1024]{2,1,0:T(8,128)(2,1)} %get-tuple-element.369, bf16[1,4096,1024]{2,1,0:T(8,128)(2,1)} %get-tuple-element.373, bf16[128,1024]{1,0:T(8,128)(2,1)S(1)} %get-tuple-element.372, bf16[2,128,4096]{2,1,0:T(8,128)(2,1)} %get-tuple-element.370, ...), kind=kOutput, calls=%fused_computation.24 | convolution fusion | flops 1111490560 | bytes 34865664 | tf_op jit(solution)/shard_map/while/body/eval_jaxpr/cond/branch_1_fun/gtc,gth->gch/dot_general | solution.py:148
  601.2 12.2 %subtract_bitcast_fusion = f32[1024,4096]{1,0:T(8,128)} fusion(bf16[1,1024,4096]{2,1,0:T(8,128)(2,1)} %get-tuple-element.414, bf16[1,1024,4096]{2,1,0:T(8,128)(2,1)} %get-tuple-element.413), kind=kLoop, calls=%fused_computation.47 | loop fusion | flops 12582912 | bytes 33554432 | tf_op jit(solution)/shard_map/reduce_sum | solution.py:187
  613.4 13.2 %subtract_bitcast_fusion.1 = f32[4096,1024]{1,0:T(8,128)} fusion(bf16[1,4096,1024]{2,1,0:T(8,128)(2,1)} %get-tuple-element.412, bf16[1,4096,1024]{2,1,0:T(8,128)(2,1)} %get-tuple-element.411), kind=kLoop, calls=%fused_computation.48 | loop fusion | flops 12582912 | bytes 33554432 | tf_op jit(solution)/shard_map/reduce_sum | solution.py:186
  626.7 96.6 %reduce-scatter.5.cloned.1.call-done = f32[1024,256]{1,0:T(8,128)} async-done(((f32[1024,4096]{1,0:T(8,128)}), f32[1024,256]{1,0:T(8,128)}) %reduce-scatter.5.cloned.1.call-update) | async-done | bytes 1048592 | tf_op jit(solution)/shard_map/reduce_scatter | solution.py:190
  725.3 111.5 %reduce-scatter.3.cloned.1.call-done = f32[256,1024]{1,0:T(8,128)} async-done(((f32[4096,1024]{1,0:T(8,128)}), f32[256,1024]{1,0:T(8,128)}) %reduce-scatter.3.cloned.1.call-update) | async-done | bytes 1048592 | tf_op jit(solution)/shard_map/reduce_scatter | solution.py:189
  (144 shorter events, 229.6 us)
Async XLA Ops:
  7.2 117.9 %all-gather.10.cloned.1.call-start = ((), (), s32[]{:S(2)}) async-start(), calls=%async_computation.2 | async-start | bytes 17825792 | tf_op jit(solution)/shard_map/all_gather | solution.py:17
  151.0 36.8 %all-gather.12.cloned.1.call-start = ((), (), s32[]{:S(2)}) async-start(), calls=%async_computation.5 | async-start | bytes 2621440 | tf_op jit(solution)/shard_map/while/body/eval_jaxpr/all_gather | solution.py:26
  195.4 24.1 %collective-permute-start = (bf16[128,4096]{1,0:T(8,128)(2,1)}, bf16[128,4096]{1,0:T(8,128)(2,1)S(1)}, u32[]{:S(2)}, u32[]{:S(2)}) collective-permute-start(bf16[128,4096]{1,0:T(8,128)(2,1)} %get-tuple-element.782), channel_id=1, source_target_pairs={{0,64},{1,65},{2,66},{3,67},{4,68},{5,69},{6,70},{7,71},{8,72},{9,... | collective-permute-start | bytes 3145736 | tf_op jit(solution)/shard_map/while/body/eval_jaxpr/ppermute | solution.py:32
  220.4 38.2 %all-gather.12.cloned.1.call-start = ((), (), s32[]{:S(2)}) async-start(), calls=%async_computation.5 | async-start | bytes 2621440 | tf_op jit(solution)/shard_map/while/body/eval_jaxpr/all_gather | solution.py:26
  266.2 24.7 %collective-permute-start = (bf16[128,4096]{1,0:T(8,128)(2,1)}, bf16[128,4096]{1,0:T(8,128)(2,1)S(1)}, u32[]{:S(2)}, u32[]{:S(2)}) collective-permute-start(bf16[128,4096]{1,0:T(8,128)(2,1)} %get-tuple-element.782), channel_id=1, source_target_pairs={{0,64},{1,65},{2,66},{3,67},{4,68},{5,69},{6,70},{7,71},{8,72},{9,... | collective-permute-start | bytes 3145736 | tf_op jit(solution)/shard_map/while/body/eval_jaxpr/ppermute | solution.py:32
  291.9 39.1 %all-gather.12.cloned.1.call-start = ((), (), s32[]{:S(2)}) async-start(), calls=%async_computation.5 | async-start | bytes 2621440 | tf_op jit(solution)/shard_map/while/body/eval_jaxpr/all_gather | solution.py:26
  334.0 29.3 %collective-permute-start = (bf16[128,4096]{1,0:T(8,128)(2,1)}, bf16[128,4096]{1,0:T(8,128)(2,1)S(1)}, u32[]{:S(2)}, u32[]{:S(2)}) collective-permute-start(bf16[128,4096]{1,0:T(8,128)(2,1)} %get-tuple-element.782), channel_id=1, source_target_pairs={{0,64},{1,65},{2,66},{3,67},{4,68},{5,69},{6,70},{7,71},{8,72},{9,... | collective-permute-start | bytes 3145736 | tf_op jit(solution)/shard_map/while/body/eval_jaxpr/ppermute | solution.py:32
  364.3 8.8 copy-start.4
  382.1 38.7 %all-gather.14.cloned.1.call-start = ((), (), s32[]{:S(2)}) async-start(), calls=%async_computation.6 | async-start | bytes 2621440 | tf_op jit(solution)/shard_map/while/body/eval_jaxpr/all_gather | solution.py:26
  384.7 37.9 %copy-start.5 = (f32[2,128,1024]{2,1,0:T(8,128)S(1)}, f32[2,128,1024]{2,1,0:T(8,128)}, u32[]{:S(2)}) copy-start(f32[2,128,1024]{2,1,0:T(8,128)} %get-tuple-element.773) | copy-start | bytes 3145732 | tf_op jit(solution)/shard_map/while
  423.9 31.2 %collective-permute-start.1 = (bf16[128,4096]{1,0:T(8,128)(2,1)}, bf16[128,4096]{1,0:T(8,128)(2,1)S(1)}, u32[]{:S(2)}, u32[]{:S(2)}) collective-permute-start(bf16[128,4096]{1,0:T(8,128)(2,1)} %copy-done.7), channel_id=1, source_target_pairs={{64,0},{65,1},{66,2},{67,3},{68,4},{69,5},{70,6},{71,7},{72,8},{73... | collective-permute-start | bytes 3145736 | tf_op jit(solution)/shard_map/while/body/eval_jaxpr/ppermute | solution.py:32
  455.1 37.9 %all-gather.14.cloned.1.call-start = ((), (), s32[]{:S(2)}) async-start(), calls=%async_computation.6 | async-start | bytes 2621440 | tf_op jit(solution)/shard_map/while/body/eval_jaxpr/all_gather | solution.py:26
  457.7 37.1 %copy-start.5 = (f32[2,128,1024]{2,1,0:T(8,128)S(1)}, f32[2,128,1024]{2,1,0:T(8,128)}, u32[]{:S(2)}) copy-start(f32[2,128,1024]{2,1,0:T(8,128)} %get-tuple-element.773) | copy-start | bytes 3145732 | tf_op jit(solution)/shard_map/while
  502.3 26.9 %collective-permute-start.1 = (bf16[128,4096]{1,0:T(8,128)(2,1)}, bf16[128,4096]{1,0:T(8,128)(2,1)S(1)}, u32[]{:S(2)}, u32[]{:S(2)}) collective-permute-start(bf16[128,4096]{1,0:T(8,128)(2,1)} %copy-done.7), channel_id=1, source_target_pairs={{64,0},{65,1},{66,2},{67,3},{68,4},{69,5},{70,6},{71,7},{72,8},{73... | collective-permute-start | bytes 3145736 | tf_op jit(solution)/shard_map/while/body/eval_jaxpr/ppermute | solution.py:32
  503.6 12.9 %copy-start = (bf16[1,1024,4096]{2,1,0:T(8,128)(2,1)S(1)}, bf16[1,1024,4096]{2,1,0:T(8,128)(2,1)}, u32[]{:S(2)}) copy-start(bf16[1,1024,4096]{2,1,0:T(8,128)(2,1)} %get-tuple-element.374) | copy-start | bytes 25165828 | tf_op jit(solution)/shard_map/while/body/eval_jaxpr/cond
  525.8 3.4 copy-start.1
  529.1 35.9 %all-gather.14.cloned.1.call-start = ((), (), s32[]{:S(2)}) async-start(), calls=%async_computation.6 | async-start | bytes 2621440 | tf_op jit(solution)/shard_map/while/body/eval_jaxpr/all_gather | solution.py:26
  531.7 35.1 %copy-start.5 = (f32[2,128,1024]{2,1,0:T(8,128)S(1)}, f32[2,128,1024]{2,1,0:T(8,128)}, u32[]{:S(2)}) copy-start(f32[2,128,1024]{2,1,0:T(8,128)} %get-tuple-element.773) | copy-start | bytes 3145732 | tf_op jit(solution)/shard_map/while
  573.3 1.0 copy-start.7
  574.3 26.9 %collective-permute-start.1 = (bf16[128,4096]{1,0:T(8,128)(2,1)}, bf16[128,4096]{1,0:T(8,128)(2,1)S(1)}, u32[]{:S(2)}, u32[]{:S(2)}) collective-permute-start(bf16[128,4096]{1,0:T(8,128)(2,1)} %copy-done.7), channel_id=1, source_target_pairs={{64,0},{65,1},{66,2},{67,3},{68,4},{69,5},{70,6},{71,7},{72,8},{73... | collective-permute-start | bytes 3145736 | tf_op jit(solution)/shard_map/while/body/eval_jaxpr/ppermute | solution.py:32
  575.6 12.9 %copy-start = (bf16[1,1024,4096]{2,1,0:T(8,128)(2,1)S(1)}, bf16[1,1024,4096]{2,1,0:T(8,128)(2,1)}, u32[]{:S(2)}) copy-start(bf16[1,1024,4096]{2,1,0:T(8,128)(2,1)} %get-tuple-element.374) | copy-start | bytes 25165828 | tf_op jit(solution)/shard_map/while/body/eval_jaxpr/cond
  597.8 3.4 copy-start.1
  601.2 122.1 %reduce-scatter.5.cloned.1.call-start = ((), (), s32[]{:S(2)}) async-start(), calls=%async_computation.4 | async-start | bytes 17825792 | tf_op jit(solution)/shard_map/reduce_scatter | solution.py:190
  613.4 223.4 %reduce-scatter.3.cloned.1.call-start = ((), (), s32[]{:S(2)}) async-start(), calls=%async_computation.3 | async-start | bytes 17825792 | tf_op jit(solution)/shard_map/reduce_scatter | solution.py:189
  (11 other events, 9.6 us)
Sparse Core Ops, SparseCore 0:
  10.7 114.3 all-gather.9
  161.0 26.7 all-gather.11
  230.5 28.0 all-gather.11
  297.3 33.5 all-gather.11
  385.8 34.9 all-gather.13
  465.0 27.9 all-gather.13
  539.0 25.9 all-gather.13
  613.5 109.7 reduce-scatter.4
  726.7 110.0 reduce-scatter.2
where the time goes:
time: 890 us; the launch traced here: 885 us
  waiting for transfers between devices  598 us (67%)
  matrix products  90.1 us (10%)
  local copies, waits for them, and re-layouts  66.9 us (8%)
  other arithmetic  62.4 us (7%)
  blocking collectives  32.1 us (4%)
  between operations  17 us (2%)
  starting transfers between devices  14.4 us (2%)
    all_gather x6, waiting for transfers between devices, total_of_pieces(): return lax.all_gather(value, axis).sum(0)  178 us
    all_gather x1, waiting for transfers between devices, rows_first(): filled, at, done = (lax.all_gather(both, axis, axis=0, tiled=True), 0, [])  115 us
    reduce_scatter x1, waiting for transfers between devices, on_device(): lax.psum_scatter(total_in, DP, scatter_dimension=0, tiled=True)  111 us
    ppermute x6, waiting for transfers between devices, from_behind(): return lax.ppermute(value, axis, pairs)  96.7 us
    reduce_scatter x1, waiting for transfers between devices, on_device(): lax.psum_scatter(total_out, DP, scatter_dimension=1, tiled=True)  96.6 us
    psum x5, blocking collectives, by_axis(): value = lax.psum(value, axis)  32.1 us
    dot_general x2, matrix products, accumulate(): jnp.einsum('gtc,gth->gch', x_groups, slope_groups, preferred_element_type...  25.8 us
    dot_general x4, matrix products, contract_last(): lax.dot_general(first_operand, second_operand, (((1,), (1,)), ((), ())),...  25.2 us
  transfers between devices with their start and end apart: 15, of which 13 were waited for; matrix products, arithmetic and copies ran while one was open for 7% of the time, Pallas kernels for 0%

commit v1 on v0

v1 whole, which is shorter than its diff:
```python
import jax
import jax.numpy as jnp
from jax import lax
from jax.experimental import pallas as pl
from jax.experimental.pallas import tpu as pltpu
from jax.sharding import Mesh
from jax.sharding import PartitionSpec as P

CLIP_NORM = 16384.0
AXES = ("pipe", "xhi", "core", "z", "y")
TENSOR = ("xhi", "core")
DP = ("z", "y")
PIPE_TENSOR_DP = ("pipe", "xhi", "core", "z", "y")
TENSOR_DP = ("xhi", "core", "z", "y")
MESH = pl.DeviceIdType.MESH
BF = jnp.bfloat16
F32 = jnp.float32

RING = 4
REP = RING * RING
GROUP = 8
NT = (((1,), (1,)), ((), ()))
TN = (((0,), (0,)), ((), ()))


def kernel(
    x_hbm, win_hbm, wot_hbm, cot_hbm,
    upd_in, upd_out, norm_out,
    x0, cot, x1, err1, w, g, act, slope, part, xrecv, r1a, r1b, r2a, r2b,
    fin, pex, prx, nsum, nz, ny, nx, pre_keep,
    lsem, ssem, rsem,
):
    micro, tok, half_d = x0.shape
    rows = micro * tok
    hid = w.shape[-1]
    sub = w.shape[3]
    hl = hid // 2
    chunk = rows // GROUP
    pipe = lax.axis_index("pipe")
    xhi = lax.axis_index("xhi")
    core = lax.axis_index("core")
    z = lax.axis_index("z")
    y = lax.axis_index("y")
    other = 1 - pipe
    c_me = pipe * 4 + xhi * 2 + core

    def turn(v, d):
        return lax.rem(v + d, RING)

    started = []
    count = [0]
    lcount = [0]

    def remote(src, dst, dev):
        i = count[0]
        count[0] += 1
        copy = pltpu.make_async_remote_copy(
            src_ref=src, dst_ref=dst, send_sem=ssem.at[i], recv_sem=rsem.at[i],
            device_id=dev, device_id_type=MESH,
        )
        copy.start()
        started.append(copy)
        return copy

    def local(src, dst):
        i = lcount[0]
        lcount[0] += 1
        copy = pltpu.make_async_copy(src, dst, lsem.at[i])
        copy.start()
        return copy

    def wait_all(copies):
        for copy in copies:
            copy.wait_recv()

    xpeers = []
    for code in range(1, GROUP):
        a, b, c = code // 4, (code // 2) % 2, code % 2
        p_ = other if a else pipe
        h_ = 1 - xhi if b else xhi
        c_ = 1 - core if c else core
        xpeers.append((code, {"pipe": p_, "xhi": h_, "core": c_}, p_ * 4 + h_ * 2 + c_))

    own_w = [
        local(win_hbm.at[pl.ds(pl.multiple_of(pipe * sub, sub), sub), :], w.at[2 * pipe, z, y]),
        local(wot_hbm.at[pl.ds(pl.multiple_of(pipe * sub, sub), sub), :], w.at[2 * pipe + 1, z, y]),
    ]
    loads = {}
    for name, src, dst in (("x", x_hbm, x0), ("cot", cot_hbm, cot)):
        loads[name] = []
        for r in range(REP):
            off = pl.multiple_of(r * 2 * sub + pipe * sub, sub)
            loads[name].append(
                local(src.at[:, :, pl.ds(off, sub)], dst.at[:, :, pl.ds(r * sub, sub)])
            )

    barrier = pltpu.get_barrier_semaphore()
    peers = [dev for _, dev, _ in xpeers]
    for d in range(1, RING):
        peers.append({"z": turn(z, d)})
        peers.append({"y": turn(y, d)})
    for dev in peers:
        pl.semaphore_signal(barrier, inc=1, device_id=dev, device_id_type=MESH)
    pl.semaphore_wait(barrier, len(peers))

    pair = {"pipe": other}
    give = []
    for kind, src in ((0, win_hbm), (1, wot_hbm)):
        give.append(
            remote(
                src.at[pl.ds(pl.multiple_of(other * sub, sub), sub), :],
                w.at[2 * pipe + kind, z, y],
                pair,
            )
        )

    A, B = pl.ds(0, hl), pl.ds(hl, hl)
    up_z, dn_z = {"z": turn(z, 1)}, {"z": turn(z, 3)}
    up_y, dn_y = {"y": turn(y, 1)}, {"y": turn(y, 3)}
    hs = sub // 2

    def same(ref, dev):
        return remote(ref, ref, dev)

    def g1a(k):
        a, b = w.at[k, z, y, :, A], w.at[k, z, y, :, B]
        return [same(a, up_y), same(a, dn_y), same(b, up_z), same(b, dn_z)]

    def g1b(k):
        return [
            same(w.at[k, z, turn(y, 3), pl.ds(0, hs), A], up_y),
            same(w.at[k, z, turn(y, 1), pl.ds(hs, hs), A], dn_y),
            same(w.at[k, turn(z, 3), y, pl.ds(0, hs), B], up_z),
            same(w.at[k, turn(z, 1), y, pl.ds(hs, hs), B], dn_z),
        ]

    def g2a(k):
        a, b = w.at[k, z, :, :, A], w.at[k, :, y, :, B]
        return [same(a, up_z), same(a, dn_z), same(b, up_y), same(b, dn_y)]

    def g2b(k):
        return [
            same(w.at[k, turn(z, 3), pl.ds(0, 2), :, A], up_z),
            same(w.at[k, turn(z, 1), pl.ds(2, 2), :, A], dn_z),
            same(w.at[k, pl.ds(0, 2), turn(y, 3), :, B], up_y),
            same(w.at[k, pl.ds(2, 2), turn(y, 1), :, B], dn_y),
        ]

    tile = 256

    def project(src, k, ph):
        @pl.loop(0, hid // tile)
        def _(n):
            cols = pl.ds(pl.multiple_of(n * tile, tile), tile)
            left = src[...].reshape(rows, half_d)
            right = w[k, :, :, :, cols].reshape(half_d, tile)
            part[ph, :, cols] = jnp.dot(left, right, preferred_element_type=F32).astype(BF)

    def widen(base, units, k, out):
        def wide(base_ref, units_ref, out_ref):
            for zz in range(RING):
                @pl.loop(0, 2)
                def _(q):
                    cols = pl.ds(pl.multiple_of(zz * 4 * sub + q * 2 * sub, tile), 2 * sub)
                    right = w[k, zz, pl.ds(q * 2, 2), :, :].reshape(2 * sub, hid)
                    add = lax.dot_general(units_ref, right, NT, preferred_element_type=F32)
                    old = base_ref[:, :, cols].reshape(rows, 2 * sub).astype(F32)
                    out_ref[:, :, cols] = (old + add).astype(BF).reshape(micro, tok, 2 * sub)

        wide(base, units[...], out)

    def weight_grad(left_ref, right, k):
        for zz in range(RING):
            @pl.loop(0, 2)
            def _(q):
                cols = pl.ds(pl.multiple_of(zz * 4 * sub + q * 2 * sub, tile), 2 * sub)
                left = left_ref[:, :, cols].reshape(rows, 2 * sub)
                got = lax.dot_general(left, right[...], TN, preferred_element_type=F32)
                g[k, zz, pl.ds(q * 2, 2), :, :] = got.astype(BF).reshape(2, sub, hid)

    def scatter_units(ph):
        copies = []
        for code, dev, c in xpeers:
            at = pl.ds(pl.multiple_of(c * chunk, chunk), chunk)
            copies.append(remote(part.at[ph, at, :], xrecv.at[ph, code], dev))
        return copies

    mine = pl.ds(pl.multiple_of(c_me * chunk, chunk), chunk)

    def units_sum(ph):
        total = part[ph, mine, :].astype(F32)
        for code in range(1, GROUP):
            total = total + xrecv[ph, code].astype(F32)
        return total

    def spread_units(ref, value):
        ref[mine, :] = value
        return [remote(ref.at[mine, :], ref.at[mine, :], dev) for _, dev, _ in xpeers]

    def slope_of(up, pre):
        s = jax.nn.sigmoid(pre)
        return (up * s * (1.0 + pre * (1.0 - s))).astype(BF)

    def s1a(k):
        z2, y2 = turn(z, 2), turn(y, 2)
        return [
            remote(g.at[k, z2, pl.ds(0, 2), :, A], r1a.at[k, 0, 0], up_z),
            remote(g.at[k, z2, pl.ds(2, 2), :, A], r1a.at[k, 0, 1], dn_z),
            remote(g.at[k, pl.ds(0, 2), y2, :, B], r1a.at[k, 1, 0], up_y),
            remote(g.at[k, pl.ds(2, 2), y2, :, B], r1a.at[k, 1, 1], dn_y),
        ]

    def s1b(k):
        zu, zd, yu, yd = turn(z, 1), turn(z, 3), turn(y, 1), turn(y, 3)

        @pl.loop(0, 2)
        def _(q):
            g[k, zu, q, :, A] = (g[k, zu, q, :, A].astype(F32) + r1a[k, 0, 0, q].astype(F32)).astype(BF)
            g[k, zd, q + 2, :, A] = (
                g[k, zd, q + 2, :, A].astype(F32) + r1a[k, 0, 1, q].astype(F32)
            ).astype(BF)
            g[k, q, yu, :, B] = (g[k, q, yu, :, B].astype(F32) + r1a[k, 1, 0, q].astype(F32)).astype(BF)
            g[k, q + 2, yd, :, B] = (
                g[k, q + 2, yd, :, B].astype(F32) + r1a[k, 1, 1, q].astype(F32)
            ).astype(BF)

        return [
            remote(g.at[k, zu, :, :, A], r1b.at[k, 0, 0], up_z),
            remote(g.at[k, zd, :, :, A], r1b.at[k, 0, 1], dn_z),
            remote(g.at[k, :, yu, :, B], r1b.at[k, 1, 0], up_y),
            remote(g.at[k, :, yd, :, B], r1b.at[k, 1, 1], dn_y),
        ]

    def s2a(k):
        @pl.loop(0, RING)
        def _(q):
            a = g[k, z, q, :, A].astype(F32) + r1b[k, 0, 0, q].astype(F32) + r1b[k, 0, 1, q].astype(F32)
            g[k, z, q, :, A] = a.astype(BF)
            b = g[k, q, y, :, B].astype(F32) + r1b[k, 1, 0, q].astype(F32) + r1b[k, 1, 1, q].astype(F32)
            g[k, q, y, :, B] = b.astype(BF)

        z2, y2 = turn(z, 2), turn(y, 2)
        return [
            remote(g.at[k, z, y2, pl.ds(0, hs), A], r2a.at[k, 0, 0], up_y),
            remote(g.at[k, z, y2, pl.ds(hs, hs), A], r2a.at[k, 0, 1], dn_y),
            remote(g.at[k, z2, y, pl.ds(0, hs), B], r2a.at[k, 1, 0], up_z),
            remote(g.at[k, z2, y, pl.ds(hs, hs), B], r2a.at[k, 1, 1], dn_z),
        ]

    def s2b(k):
        zu, zd, yu, yd = turn(z, 1), turn(z, 3), turn(y, 1), turn(y, 3)
        lo, hi = pl.ds(0, hs), pl.ds(hs, hs)
        g[k, z, yu, lo, A] = (g[k, z, yu, lo, A].astype(F32) + r2a[k, 0, 0].astype(F32)).astype(BF)
        g[k, z, yd, hi, A] = (g[k, z, yd, hi, A].astype(F32) + r2a[k, 0, 1].astype(F32)).astype(BF)
        g[k, zu, y, lo, B] = (g[k, zu, y, lo, B].astype(F32) + r2a[k, 1, 0].astype(F32)).astype(BF)
        g[k, zd, y, hi, B] = (g[k, zd, y, hi, B].astype(F32) + r2a[k, 1, 1].astype(F32)).astype(BF)
        return [
            remote(g.at[k, z, yu, :, A], r2b.at[k, 0, 0], up_y),
            remote(g.at[k, z, yd, :, A], r2b.at[k, 0, 1], dn_y),
            remote(g.at[k, zu, y, :, B], r2b.at[k, 1, 0], up_z),
            remote(g.at[k, zd, y, :, B], r2b.at[k, 1, 1], dn_z),
        ]

    def s2c(k):
        a = g[k, z, y, :, A].astype(F32) + r2b[k, 0, 0].astype(F32) + r2b[k, 0, 1].astype(F32)
        b = g[k, z, y, :, B].astype(F32) + r2b[k, 1, 0].astype(F32) + r2b[k, 1, 1].astype(F32)
        fin[k, :, A] = a
        fin[k, :, B] = b
        sq = a * a + b * b
        sq = sq.reshape(sub // 8, 8, hl).sum(0)
        total = sq[:, 0:128]
        for i in range(1, hl // 128):
            total = total + sq[:, i * 128 : (i + 1) * 128]
        return total

    def hand_over(kind):
        pex[kind] = fin[2 * other + kind].astype(BF)
        return remote(pex.at[kind], prx.at[kind], pair)

    for copy in own_w:
        copy.wait()
    give[0].wait_recv()
    c1a = {0: g1a(0)}
    wait_all(c1a[0])
    c1b = {0: g1b(0)}
    c1a[2] = g1a(2)
    give[1].wait_recv()
    c1a[1] = g1a(1)
    c1a[3] = g1a(3)
    wait_all(c1b[0])
    c2a = {0: g2a(0)}
    c2b = {}
    wait_all(c1a[1])
    c1b[1] = g1b(1)
    wait_all(c1a[2])
    c1b[2] = g1b(2)
    wait_all(c1a[3])
    c1b[3] = g1b(3)
    wait_all(c1b[1])
    c2a[1] = g2a(1)
    wait_all(c2a[0])
    c2b[0] = g2b(0)
    wait_all(c1b[2])
    c2a[2] = g2a(2)
    for copy in loads["x"]:
        copy.wait()
    wait_all(c2b[0])
    project(x0, 0, 0)
    p0 = scatter_units(0)
    wait_all(c2a[1])
    c2b[1] = g2b(1)
    wait_all(c1b[3])
    c2a[3] = g2a(3)
    wait_all(p0)
    pre0 = units_sum(0)
    pre_keep[0] = pre0
    a0 = spread_units(act.at[0], jax.nn.silu(pre0).astype(BF))
    wait_all(c2a[2])
    c2b[2] = g2b(2)
    wait_all(a0)
    wait_all(c2b[1])
    widen(x0, act.at[0], 1, x1)
    wait_all(c2b[2])
    project(x1, 2, 1)
    p1 = scatter_units(1)
    wait_all(c2a[3])
    c2b[3] = g2b(3)
    wait_all(p1)
    pre1 = units_sum(1)
    pre_keep[1] = pre1
    a1 = spread_units(act.at[1], jax.nn.silu(pre1).astype(BF))
    for copy in loads["cot"]:
        copy.wait()
    wait_all(c2b[3])
    project(cot, 3, 2)
    p2 = scatter_units(2)
    wait_all(a1)
    weight_grad(cot, act.at[1], 3)
    d1a = {3: s1a(3)}
    wait_all(p2)
    v1 = spread_units(slope.at[1], slope_of(units_sum(2), pre_keep[1]))
    d1b, d2a, d2b = {}, {}, {}
    wait_all(d1a[3])
    d1b[3] = s1b(3)
    wait_all(v1)
    weight_grad(x1, slope.at[1], 2)
    d1a[2] = s1a(2)
    widen(cot, slope.at[1], 2, err1)
    project(err1, 1, 3)
    p3 = scatter_units(3)
    weight_grad(err1, act.at[0], 1)
    d1a[1] = s1a(1)
    wait_all(p3)
    v0 = spread_units(slope.at[0], slope_of(units_sum(3), pre_keep[0]))
    wait_all(d1a[2])
    d1b[2] = s1b(2)
    wait_all(v0)
    weight_grad(x0, slope.at[0], 0)
    d1a[0] = s1a(0)
    wait_all(d1b[3])
    d2a[3] = s2a(3)
    wait_all(d1a[1])
    d1b[1] = s1b(1)
    wait_all(d2a[3])
    d2b[3] = s2b(3)
    wait_all(d1b[2])
    d2a[2] = s2a(2)
    wait_all(d1a[0])
    d1b[0] = s1b(0)
    wait_all(d2b[3])
    squares = s2c(3)
    wait_all(d2a[2])
    d2b[2] = s2b(2)
    wait_all(d1b[1])
    d2a[1] = s2a(1)
    wait_all(d2b[2])
    squares = squares + s2c(2)
    wait_all(d2a[1])
    d2b[1] = s2b(1)
    wait_all(d1b[0])
    d2a[0] = s2a(0)
    wait_all(d2b[1])
    squares = squares + s2c(1)
    h1 = hand_over(1)
    wait_all(d2a[0])
    d2b[0] = s2b(0)
    wait_all(d2b[0])
    squares = squares + s2c(0)
    h0 = hand_over(0)

    nsum[0] = squares
    nzc = [remote(nsum.at[0], nz.at[d], {"z": turn(z, d)}) for d in range(1, RING)]
    wait_all(nzc)
    nsum[1] = nsum[0] + nz[1] + nz[2] + nz[3]
    nyc = [remote(nsum.at[1], ny.at[d], {"y": turn(y, d)}) for d in range(1, RING)]
    wait_all(nyc)
    nsum[2] = nsum[1] + ny[1] + ny[2] + ny[3]
    nxc = [remote(nsum.at[2], nx.at[code], dev) for code, dev, _ in xpeers]
    wait_all(nxc)
    total = nsum[2]
    for code in range(1, GROUP):
        total = total + nx[code]
    norm = jnp.sqrt(jnp.sum(total, keepdims=True))
    norm_out[...] = jnp.broadcast_to(norm, norm_out.shape)
    factor = jnp.minimum(1.0, CLIP_NORM / norm)
    h1.wait_recv()
    h0.wait_recv()
    at_own = pl.ds(pl.multiple_of(pipe * sub, sub), sub)
    at_other = pl.ds(pl.multiple_of(other * sub, sub), sub)
    for kind, out in ((0, upd_in), (1, upd_out)):
        out[at_own, :] = fin[2 * pipe + kind] * factor
        out[at_other, :] = prx[kind].astype(F32) * factor
    for copy in started:
        copy.wait_send()


def on_device(inputs, w_in, w_out, cotangent):
    micro, tok, cols = inputs.shape
    shard, hid = w_in.shape[1], w_in.shape[2]
    sub = shard // 2
    half_d = cols // 2
    rows = micro * tok
    chunk = rows // GROUP
    hl = hid // 2
    any_spec = pl.BlockSpec(memory_space=pl.ANY)
    vmem = pl.BlockSpec(memory_space=pltpu.VMEM)
    upd_in, upd_out_t, norm = pl.pallas_call(
        kernel,
        out_shape=(
            jax.ShapeDtypeStruct((shard, hid), F32),
            jax.ShapeDtypeStruct((shard, hid), F32),
            jax.ShapeDtypeStruct((8, 128), F32),
        ),
        in_specs=[any_spec] * 4,
        out_specs=(vmem, vmem, vmem),
        scratch_shapes=[
            pltpu.VMEM((micro, tok, half_d), BF),
            pltpu.VMEM((micro, tok, half_d), BF),
            pltpu.VMEM((micro, tok, half_d), BF),
            pltpu.VMEM((micro, tok, half_d), BF),
            pltpu.VMEM((4, RING, RING, sub, hid), BF),
            pltpu.VMEM((4, RING, RING, sub, hid), BF),
            pltpu.VMEM((2, rows, hid), BF),
            pltpu.VMEM((2, rows, hid), BF),
            pltpu.VMEM((4, rows, hid), BF),
            pltpu.VMEM((4, GROUP, chunk, hid), BF),
            pltpu.VMEM((4, 2, 2, 2, sub, hl), BF),
            pltpu.VMEM((4, 2, 2, RING, sub, hl), BF),
            pltpu.VMEM((4, 2, 2, sub // 2, hl), BF),
            pltpu.VMEM((4, 2, 2, sub, hl), BF),
            pltpu.VMEM((4, sub, hid), F32),
            pltpu.VMEM((2, sub, hid), BF),
            pltpu.VMEM((2, sub, hid), BF),
            pltpu.VMEM((3, 8, 128), F32),
            pltpu.VMEM((RING, 8, 128), F32),
            pltpu.VMEM((RING, 8, 128), F32),
            pltpu.VMEM((GROUP, 8, 128), F32),
            pltpu.VMEM((2, chunk, hid), F32),
            pltpu.SemaphoreType.DMA((40,)),
            pltpu.SemaphoreType.DMA((220,)),
            pltpu.SemaphoreType.DMA((220,)),
        ],
        compiler_params=pltpu.CompilerParams(
            collective_id=0, has_side_effects=True, vmem_limit_bytes=67043328
        ),
    )(inputs, w_in[0], w_out[0].T, cotangent)
    return upd_in[None], upd_out_t.T[None], norm[0, 0]


def solution(mesh):
    split = Mesh(mesh.devices.reshape(mesh.shape["pipe"], 2, 2, RING, RING), AXES)
    placed = (
        P(None, DP, TENSOR),
        P("pipe", TENSOR_DP, None),
        P("pipe", None, TENSOR_DP),
        P(None, DP, TENSOR),
    )
    return jax.shard_map(
        on_device,
        mesh=split,
        in_specs=placed,
        out_specs=(P("pipe", TENSOR_DP, None), P("pipe", None, TENSOR_DP), P()),
        check_vma=False,
    )
```

time: 890 us -> 232 us (0.26)
  waiting for transfers between devices: 598 us -> 0 us
  Pallas kernels: 0 us -> 225 us
  matrix products: 90.1 us -> 0 us
  other arithmetic: 62.4 us -> 0 us
  local copies, waits for them, and re-layouts: 66.9 us -> 6.83 us
  blocking collectives: 32.1 us -> 0 us
  between operations: 17 us -> 0.65 us
  starting transfers between devices: 14.4 us -> 0 us
    all_gather x7 -> x0, waiting for transfers between devices: 293 us -> none  [the longest x6 178 us: total_of_pieces(): return lax.all_gather(value, axis).sum(0)]
    pallas_call x0 -> x1, Pallas kernels: none -> 225 us  [on_device(): pl.pallas_call(kernel, out_shape=(jax.ShapeDtypeStruct((shard, hid), F32)...]
    reduce_scatter x2 -> x0, waiting for transfers between devices: 208 us -> none  [the longest x1 111 us: on_device(): lax.psum_scatter(total_in, DP, scatter_dimension=0, tiled=True)]
    ppermute x6 -> x0, waiting for transfers between devices: 96.7 us -> none  [from_behind(): return lax.ppermute(value, axis, pairs)]
    dot_general x12 -> x0, matrix products: 90.1 us -> none  [the longest x2 25.8 us: accumulate(): jnp.einsum('gtc,gth->gch', x_groups, slope_groups, preferred_element_type...]
    reduce_sum x10 -> x0, other arithmetic: 40.4 us -> none  [the longest x1 13.2 us: on_device(): jnp.sum(sum_in.astype(jnp.float32) - err_in.astype(jnp.float32), axis=0)]
    psum x5 -> x0, blocking collectives: 32.1 us -> none  [by_axis(): value = lax.psum(value, axis)]
    while x31 -> x0, local copies, waits for them, and re-layouts: 21.9 us -> none  [the longest x1 11.3 us: on_device(): lax.scan(backward_step, (zero_rows, sums_init), jnp.arange(step_count))]
  transfers between devices with their start and end apart: 15 -> 0, of which waited for: 13 -> 0; matrix products, arithmetic and copies ran while one was open for 7% -> 0% of each run, Pallas kernels for 0% -> 0%
where the time goes in v1:
time: 232 us
  Pallas kernels  225 us (97%)
  local copies, waits for them, and re-layouts  6.83 us (3%)
    pallas_call x1, Pallas kernels, on_device(): pl.pallas_call(kernel, out_shape=(jax.ShapeDtypeStruct((shard, hid), F32)...  225 us
    unnamed x5, local copies, waits for them, and re-layouts  5.55 us

profile of v1, /device:TPU:1, one launch (start us, length us, event | category | flops | bytes accessed | tf_op | source)
XLA Modules:
  0.0 232.1 jit_solution(9735656448852833385)
XLA Ops:
  0.6 2.0 copy.7
  2.7 224.6 %shard_map.67 = (f32[256,1024]{1,0:T(8,128)}, f32[256,1024]{1,0:T(8,128)}, f32[8,128]{1,0:T(8,128)}) custom-call(bf16[2,128,4096]{2,1,0:T(8,128)(2,1)} %x_hbm.1, bf16[256,1024]{1,0:T(8,128)(2,1)} %bitcast.12, bf16[256,1024]{1,0:T(8,128)(2,1)} %bitcast.9, bf16[2,128,4096]{2,1,0:T(8,128)(2,1)} %cot_hbm.1), custom_call_target="tpu_custom_call" | custom-call | tf_op jit(solution)/shard_map/pallas_call | solution.py:427
  227.3 0.0 copy-start
  227.3 1.3 slice.3
  228.6 2.5 %copy.8 = f32[1,1024,256]{2,1,0:T(8,128)} copy(f32[1,1024,256]{1,2,0:T(8,128)} %bitcast.11) | data formatting | bytes 2097152
  231.1 0.0 copy-done
  231.1 1.0 copy.10
Async XLA Ops:
  227.3 3.8 %copy-start = (f32[256,1024]{1,0:T(8,128)S(1)}, f32[256,1024]{1,0:T(8,128)}, u32[]{:S(2)}) copy-start(f32[256,1024]{1,0:T(8,128)} %get-tuple-element.6) | copy-start | bytes 3145732

commit v2 on v1

v2 whole, which is shorter than its diff:
```python
import jax
import jax.numpy as jnp
from jax import lax
from jax.experimental import pallas as pl
from jax.experimental.pallas import tpu as pltpu
from jax.sharding import Mesh
from jax.sharding import PartitionSpec as P

CLIP_NORM = 16384.0
AXES = ("pipe", "xhi", "core", "z", "y")
TENSOR = ("xhi", "core")
DP = ("z", "y")
PIPE_TENSOR_DP = ("pipe", "xhi", "core", "z", "y")
TENSOR_DP = ("xhi", "core", "z", "y")
MESH = pl.DeviceIdType.MESH
BF = jnp.bfloat16
F32 = jnp.float32

RING = 4
GROUP = 8
NT = (((1,), (1,)), ((), ()))
TN = (((0,), (0,)), ((), ()))


def kernel(
    x_hbm, win_hbm, wot_hbm, cot_hbm,
    upd_in, upd_out, norm_out,
    x0, cot, x1, err1, w, g, act, slope,
    pown, psend, crecv, xs, xrecv, pre_keep,
    ra1, ra2, ra3, rb1, rb2, rb3,
    fin, pex, prx, nsum, n1, n2,
    lsem, ssem, rsem,
):
    tok2, hid = pown.shape[1], pown.shape[2]
    sub = w.shape[3]
    la = ra3.shape[-1]
    lb = hid - la
    chunk = tok2 // GROUP
    hs = sub // 2
    pipe = lax.axis_index("pipe")
    xhi = lax.axis_index("xhi")
    core = lax.axis_index("core")
    z = lax.axis_index("z")
    y = lax.axis_index("y")
    other = 1 - pipe
    u = y // 2
    s = lax.rem(y, 2)
    q = lax.rem(y + u, 2)
    v_oth = 1 - u
    y_ag = 3 - y
    y_tp = 4 * u + 1 - y
    e_me = pipe * 4 + xhi * 2 + s

    def turn(v, d):
        return lax.rem(v + d, RING)

    started = []
    count = [0]
    lcount = [0]

    def remote(src, dst, dev):
        i = count[0]
        count[0] += 1
        copy = pltpu.make_async_remote_copy(
            src_ref=src, dst_ref=dst, send_sem=ssem.at[i], recv_sem=rsem.at[i],
            device_id=dev, device_id_type=MESH,
        )
        copy.start()
        started.append(copy)
        return copy

    def local(src, dst):
        i = lcount[0]
        lcount[0] += 1
        copy = pltpu.make_async_copy(src, dst, lsem.at[i])
        copy.start()
        return copy

    def wait_all(copies):
        for copy in copies:
            copy.wait_recv()

    xpeers = []
    for code in (7, 6, 5, 4, 3, 2, 1):
        a, b, c = code // 4, (code // 2) % 2, code % 2
        p_ = other if a else pipe
        h_ = 1 - xhi if b else xhi
        y_, s_ = (y_tp, 1 - s) if c else (y, s)
        xpeers.append((code, {"pipe": p_, "xhi": h_, "y": y_}, p_ * 4 + h_ * 2 + s_))
    wide_peers = []
    for code in range(1, 16):
        d, b, c = code // 4, (code // 2) % 2, code % 2
        wide_peers.append(
            (code, {"z": turn(z, d), "y": y_ag if b else y, "core": 1 - core if c else core})
        )
    twin = {"core": 1 - core}
    pair = {"pipe": other}

    own_w = [
        local(win_hbm.at[pl.ds(pl.multiple_of(pipe * sub, sub), sub), :], w.at[2 * pipe, z, u]),
        local(wot_hbm.at[pl.ds(pl.multiple_of(pipe * sub, sub), sub), :], w.at[2 * pipe + 1, z, u]),
    ]

    def columns(zz, vv, qq):
        member = zz * RING + (qq + vv * (3 - 2 * qq))
        return pl.ds(pl.multiple_of(member * 2 * sub + pipe * sub, sub), sub)

    loads = {}
    for name, src, dst in (("x", x_hbm, x0), ("cot", cot_hbm, cot)):
        loads[name] = [
            local(src.at[:, :, columns(zz, vv, q)], dst.at[s, :, :, pl.ds((zz * 2 + vv) * sub, sub)])
            for zz in range(RING)
            for vv in range(2)
        ]

    barrier = pltpu.get_barrier_semaphore()
    peers = [dev for _, dev, _ in xpeers] + [dev for _, dev in wide_peers]
    for dev in peers:
        pl.semaphore_signal(barrier, inc=1, device_id=dev, device_id_type=MESH)
    pl.semaphore_wait(barrier, len(peers))

    give = []
    for kind, src in ((0, win_hbm), (1, wot_hbm)):
        give.append(
            remote(
                src.at[pl.ds(pl.multiple_of(other * sub, sub), sub), :],
                w.at[2 * pipe + kind, z, u],
                pair,
            )
        )
    swaps = {}
    for name, src, dst in (("x", x_hbm, x0), ("cot", cot_hbm, cot)):
        swaps[name] = [
            remote(
                src.at[:, :, columns(zz, vv, 1 - q)],
                dst.at[s, :, :, pl.ds((zz * 2 + vv) * sub, sub)],
                {"y": y_tp},
            )
            for zz in range(RING)
            for vv in range(2)
        ]

    A, B = pl.ds(0, la), pl.ds(la, lb)
    up, dn, ag = {"z": turn(z, 1)}, {"z": turn(z, 3)}, {"y": y_ag}
    zu, zd, z2 = turn(z, 1), turn(z, 3), turn(z, 2)
    lo, hi = pl.ds(0, hs), pl.ds(hs, hs)

    def same(ref, dev):
        return remote(ref, ref, dev)

    def ga1(k):
        return [same(w.at[k, z, u, :, A], ag)]

    def ga2(k):
        ref = w.at[k, z, :, :, A]
        return [same(ref, up), same(ref, dn)]

    def ga3(k):
        return [same(w.at[k, zd, 0, :, A], up), same(w.at[k, zu, 1, :, A], dn)]

    def gb1(k):
        ref = w.at[k, z, u, :, B]
        return [same(ref, up), same(ref, dn)]

    def gb2(k):
        return [same(w.at[k, zd, u, lo, B], up), same(w.at[k, zu, u, hi, B], dn)]

    def gb3(k):
        return [same(w.at[k, :, u, :, B], ag)]

    tile = 256

    def project(src, k, ph):
        def half(which, emit):
            @pl.loop(0, hid // tile)
            def _(n):
                cols = pl.ds(pl.multiple_of(n * tile, tile), tile)
                left = src[which].reshape(tok2, src.shape[-1])
                right = w[k, :, :, :, cols].reshape(src.shape[-1], tile)
                emit(cols, jnp.dot(left, right, preferred_element_type=F32))

        def emit_send(cols, value):
            psend[ph, :, cols] = value.astype(BF)

        def emit_own(cols, value):
            pown[ph, :, cols] = value

        half(1 - core, emit_send)
        copy = remote(psend.at[ph], crecv.at[ph], twin)
        half(core, emit_own)
        return copy

    def widen(base, units, k, out):
        @pl.loop(0, RING)
        def _(zz):
            cols = pl.ds(pl.multiple_of(zz * 2 * sub, 2 * sub), 2 * sub)
            left = units[...].reshape(2 * tok2, hid)
            right = w[k, zz].reshape(2 * sub, hid)
            add = lax.dot_general(left, right, NT, preferred_element_type=F32)
            old = base[:, :, :, cols].reshape(2 * tok2, 2 * sub).astype(F32)
            out[:, :, :, cols] = (old + add).astype(BF).reshape(2, 2, tok2 // 2, 2 * sub)

    def weight_grad(left_ref, right, k):
        @pl.loop(0, RING)
        def _(zz):
            cols = pl.ds(pl.multiple_of(zz * 2 * sub, 2 * sub), 2 * sub)
            left = left_ref[:, :, :, cols].reshape(2 * tok2, 2 * sub)
            units = right[...].reshape(2 * tok2, hid)
            got = lax.dot_general(left, units, TN, preferred_element_type=F32)
            g[k, zz] = got.astype(BF).reshape(2, sub, hid)

    def scatter_units(ph, copy):
        copy.wait_recv()
        copies = []
        for code, dev, e in xpeers:
            at = pl.ds(pl.multiple_of(e * chunk, chunk), chunk)
            xs[ph, code] = (pown[ph, at, :] + crecv[ph, at, :].astype(F32)).astype(BF)
            copies.append(remote(xs.at[ph, code], xrecv.at[ph, code], dev))
        return copies

    mine = pl.ds(pl.multiple_of(e_me * chunk, chunk), chunk)

    def units_sum(ph):
        total = pown[ph, mine, :] + crecv[ph, mine, :].astype(F32)
        for code in range(1, GROUP):
            total = total + xrecv[ph, code].astype(F32)
        return total

    def spread_units(ref, value):
        ref[core, mine, :] = value
        at = ref.at[core, mine, :]
        return [remote(at, at, dev) for _, dev, _ in xpeers]

    def spread_core(ref, copies):
        wait_all(copies)
        return [same(ref.at[core], twin)]

    def slope_of(upward, pre):
        sig = jax.nn.sigmoid(pre)
        return (upward * sig * (1.0 + pre * (1.0 - sig))).astype(BF)

    def plus(x, *more):
        total = x.astype(F32)
        for m in more:
            total = total + m.astype(F32)
        return total

    def sa1(k):
        return [
            remote(g.at[k, z2, 0, :, A], ra1.at[k, 0], up),
            remote(g.at[k, z2, 1, :, A], ra1.at[k, 1], dn),
        ]

    def sa2(k):
        g[k, zu, 0, :, A] = plus(g[k, zu, 0, :, A], ra1[k, 0]).astype(BF)
        g[k, zd, 1, :, A] = plus(g[k, zd, 1, :, A], ra1[k, 1]).astype(BF)
        return [
            remote(g.at[k, zu, :, :, A], ra2.at[k, 0], up),
            remote(g.at[k, zd, :, :, A], ra2.at[k, 1], dn),
        ]

    def sa3(k):
        g[k, z, v_oth, :, A] = plus(g[k, z, v_oth, :, A], ra2[k, 0, v_oth], ra2[k, 1, v_oth]).astype(BF)
        return [remote(g.at[k, z, v_oth, :, A], ra3.at[k], ag)]

    def sb1(k):
        return [remote(g.at[k, :, v_oth, :, B], rb1.at[k], ag)]

    def sb2(k):
        @pl.loop(0, RING)
        def _(zz):
            g[k, zz, u, :, B] = plus(g[k, zz, u, :, B], rb1[k, zz]).astype(BF)

        return [
            remote(g.at[k, z2, u, lo, B], rb2.at[k, 0], up),
            remote(g.at[k, z2, u, hi, B], rb2.at[k, 1], dn),
        ]

    def sb3(k):
        g[k, zu, u, lo, B] = plus(g[k, zu, u, lo, B], rb2[k, 0]).astype(BF)
        g[k, zd, u, hi, B] = plus(g[k, zd, u, hi, B], rb2[k, 1]).astype(BF)
        return [
            remote(g.at[k, zu, u, :, B], rb3.at[k, 0], up),
            remote(g.at[k, zd, u, :, B], rb3.at[k, 1], dn),
        ]

    def fold(value):
        lanes = value.shape[-1]
        value = value.reshape(sub // 8, 8, lanes).sum(0)
        total = value[:, 0:128]
        for i in range(1, lanes // 128):
            total = total + value[:, i * 128 : (i + 1) * 128]
        return total

    def finish(k):
        a = plus(g[k, z, u, :, A], ra2[k, 0, u], ra2[k, 1, u], ra3[k])
        fin[k, :, A] = a
        b = plus(g[k, z, u, :, B], rb3[k, 0], rb3[k, 1])
        fin[k, :, B] = b
        return fold(a * a) + fold(b * b)

    def hand_over(kind):
        pex[kind] = fin[2 * other + kind].astype(BF)
        return remote(pex.at[kind], prx.at[kind], pair)

    ca1, ca2, ca3, cb1, cb2, cb3 = {}, {}, {}, {}, {}, {}
    for copy in own_w:
        copy.wait()
    give[0].wait_recv()
    ca1[0], cb1[0] = ga1(0), gb1(0)
    ca1[2], cb1[2] = ga1(2), gb1(2)
    wait_all(ca1[0])
    ca2[0] = ga2(0)
    wait_all(cb1[0])
    cb2[0] = gb2(0)
    wait_all(cb2[0])
    cb3[0] = gb3(0)
    give[1].wait_recv()
    ca1[1], cb1[1] = ga1(1), gb1(1)
    ca1[3], cb1[3] = ga1(3), gb1(3)
    wait_all(ca2[0])
    ca3[0] = ga3(0)
    wait_all(cb1[2])
    cb2[2] = gb2(2)
    wait_all(cb1[1])
    cb2[1] = gb2(1)
    wait_all(ca1[1])
    ca2[1] = ga2(1)
    for copy in loads["x"]:
        copy.wait()
    wait_all(swaps["x"])
    wait_all(ca3[0])
    wait_all(cb3[0])
    cp0 = project(x0, 0, 0)
    wait_all(cb2[1])
    cb3[1] = gb3(1)
    p0 = scatter_units(0, cp0)
    wait_all(ca2[1])
    ca3[1] = ga3(1)
    wait_all(ca1[2])
    ca2[2] = ga2(2)
    wait_all(cb2[2])
    cb3[2] = gb3(2)
    wait_all(cb1[3])
    cb2[3] = gb2(3)
    wait_all(p0)
    pre0 = units_sum(0)
    pre_keep[0] = pre0
    a0 = spread_units(act.at[0], jax.nn.silu(pre0).astype(BF))
    wait_all(ca2[2])
    ca3[2] = ga3(2)
    wait_all(ca1[3])
    ca2[3] = ga2(3)
    wait_all(cb2[3])
    cb3[3] = gb3(3)
    a0 = spread_core(act.at[0], a0)
    wait_all(ca3[1])
    wait_all(cb3[1])
    wait_all(a0)
    widen(x0, act.at[0], 1, x1)
    wait_all(ca3[2])
    wait_all(cb3[2])
    cp1 = project(x1, 2, 1)
    p1 = scatter_units(1, cp1)
    wait_all(ca2[3])
    ca3[3] = ga3(3)
    for copy in loads["cot"]:
        copy.wait()
    wait_all(swaps["cot"])
    wait_all(p1)
    pre1 = units_sum(1)
    pre_keep[1] = pre1
    a1 = spread_units(act.at[1], jax.nn.silu(pre1).astype(BF))
    wait_all(ca3[3])
    wait_all(cb3[3])
    cp2 = project(cot, 3, 2)
    p2 = scatter_units(2, cp2)
    a1 = spread_core(act.at[1], a1)
    wait_all(a1)
    weight_grad(cot, act.at[1], 3)
    da1, da2, da3, db1, db2, db3 = {}, {}, {}, {}, {}, {}
    da1[3], db1[3] = sa1(3), sb1(3)
    wait_all(p2)
    v1 = spread_units(slope.at[1], slope_of(units_sum(2), pre_keep[1]))
    wait_all(da1[3])
    da2[3] = sa2(3)
    wait_all(db1[3])
    db2[3] = sb2(3)
    v1 = spread_core(slope.at[1], v1)
    wait_all(v1)
    widen(cot, slope.at[1], 2, err1)
    cp3 = project(err1, 1, 3)
    p3 = scatter_units(3, cp3)
    weight_grad(x1, slope.at[1], 2)
    da1[2], db1[2] = sa1(2), sb1(2)
    weight_grad(err1, act.at[0], 1)
    da1[1], db1[1] = sa1(1), sb1(1)
    wait_all(p3)
    v0 = spread_units(slope.at[0], slope_of(units_sum(3), pre_keep[0]))
    wait_all(db2[3])
    db3[3] = sb3(3)
    wait_all(da2[3])
    da3[3] = sa3(3)
    wait_all(da1[2])
    da2[2] = sa2(2)
    wait_all(db1[2])
    db2[2] = sb2(2)
    v0 = spread_core(slope.at[0], v0)
    wait_all(v0)
    weight_grad(x0, slope.at[0], 0)
    da1[0], db1[0] = sa1(0), sb1(0)
    wait_all(da1[1])
    da2[1] = sa2(1)
    wait_all(db1[1])
    db2[1] = sb2(1)
    wait_all(db2[2])
    db3[2] = sb3(2)
    wait_all(da2[2])
    da3[2] = sa3(2)
    wait_all(da3[3])
    wait_all(db3[3])
    squares = finish(3)
    wait_all(da1[0])
    da2[0] = sa2(0)
    wait_all(db1[0])
    db2[0] = sb2(0)
    wait_all(db2[1])
    db3[1] = sb3(1)
    wait_all(da2[1])
    da3[1] = sa3(1)
    wait_all(db2[0])
    db3[0] = sb3(0)
    wait_all(da3[2])
    wait_all(db3[2])
    squares = squares + finish(2)
    wait_all(da2[0])
    da3[0] = sa3(0)
    wait_all(da3[1])
    wait_all(db3[1])
    squares = squares + finish(1)
    h1 = hand_over(1)
    wait_all(da3[0])
    wait_all(db3[0])
    squares = squares + finish(0)
    nsum[0] = squares
    c1 = [remote(nsum.at[0], n1.at[code], dev) for code, dev, _ in xpeers]
    h0 = hand_over(0)
    wait_all(c1)
    total = nsum[0]
    for code in range(1, GROUP):
        total = total + n1[code]
    nsum[1] = total
    c2 = [remote(nsum.at[1], n2.at[code], dev) for code, dev in wide_peers]
    wait_all(c2)
    total = nsum[1]
    for code in range(1, 16):
        total = total + n2[code]
    norm = jnp.sqrt(jnp.sum(total, keepdims=True))
    norm_out[...] = jnp.broadcast_to(norm, norm_out.shape)
    factor = jnp.minimum(1.0, CLIP_NORM / norm)
    h1.wait_recv()
    h0.wait_recv()
    at_own = pl.ds(pl.multiple_of(pipe * sub, sub), sub)
    at_other = pl.ds(pl.multiple_of(other * sub, sub), sub)
    for kind, out in ((0, upd_in), (1, upd_out)):
        out[at_own, :] = fin[2 * pipe + kind] * factor
        out[at_other, :] = prx[kind].astype(F32) * factor
    for copy in started:
        copy.wait_send()


def on_device(inputs, w_in, w_out, cotangent):
    micro, tok, cols = inputs.shape
    shard, hid = w_in.shape[1], w_in.shape[2]
    sub = shard // 2
    part_d = cols // 4
    rows = micro * tok
    chunk = rows // GROUP
    la = 5 * hid // 8
    lb = hid - la
    any_spec = pl.BlockSpec(memory_space=pl.ANY)
    vmem = pl.BlockSpec(memory_space=pltpu.VMEM)
    upd_in, upd_out_t, norm = pl.pallas_call(
        kernel,
        out_shape=(
            jax.ShapeDtypeStruct((shard, hid), F32),
            jax.ShapeDtypeStruct((shard, hid), F32),
            jax.ShapeDtypeStruct((8, 128), F32),
        ),
        in_specs=[any_spec] * 4,
        out_specs=(vmem, vmem, vmem),
        scratch_shapes=[
            pltpu.VMEM((2, micro, tok, part_d), BF),
            pltpu.VMEM((2, micro, tok, part_d), BF),
            pltpu.VMEM((2, micro, tok, part_d), BF),
            pltpu.VMEM((2, micro, tok, part_d), BF),
            pltpu.VMEM((4, RING, 2, sub, hid), BF),
            pltpu.VMEM((4, RING, 2, sub, hid), BF),
            pltpu.VMEM((2, 2, rows, hid), BF),
            pltpu.VMEM((2, 2, rows, hid), BF),
            pltpu.VMEM((4, rows, hid), F32),
            pltpu.VMEM((4, rows, hid), BF),
            pltpu.VMEM((4, rows, hid), BF),
            pltpu.VMEM((4, GROUP, chunk, hid), BF),
            pltpu.VMEM((4, GROUP, chunk, hid), BF),
            pltpu.VMEM((2, chunk, hid), F32),
            pltpu.VMEM((4, 2, sub, la), BF),
            pltpu.VMEM((4, 2, 2, sub, la), BF),
            pltpu.VMEM((4, sub, la), BF),
            pltpu.VMEM((4, RING, sub, lb), BF),
            pltpu.VMEM((4, 2, sub // 2, lb), BF),
            pltpu.VMEM((4, 2, sub, lb), BF),
            pltpu.VMEM((4, sub, hid), F32),
            pltpu.VMEM((2, sub, hid), BF),
            pltpu.VMEM((2, sub, hid), BF),
            pltpu.VMEM((2, 8, 128), F32),
            pltpu.VMEM((GROUP, 8, 128), F32),
            pltpu.VMEM((16, 8, 128), F32),
            pltpu.SemaphoreType.DMA((20,)),
            pltpu.SemaphoreType.DMA((200,)),
            pltpu.SemaphoreType.DMA((200,)),
        ],
        compiler_params=pltpu.CompilerParams(
            collective_id=0, has_side_effects=True, vmem_limit_bytes=67043328
        ),
    )(inputs, w_in[0], w_out[0].T, cotangent)
    return upd_in[None], upd_out_t.T[None], norm[0, 0]


def solution(mesh):
    split = Mesh(mesh.devices.reshape(mesh.shape["pipe"], 2, 2, RING, RING), AXES)
    placed = (
        P(None, DP, TENSOR),
        P("pipe", TENSOR_DP, None),
        P("pipe", None, TENSOR_DP),
        P(None, DP, TENSOR),
    )
    return jax.shard_map(
        on_device,
        mesh=split,
        in_specs=placed,
        out_specs=(P("pipe", TENSOR_DP, None), P("pipe", None, TENSOR_DP), P()),
        check_vma=False,
    )
```

time: 232 us -> 187 us (0.81)
  Pallas kernels: 225 us -> 179 us
    pallas_call x1, Pallas kernels: 225 us -> 179 us  [on_device(): pl.pallas_call(kernel, out_shape=(jax.ShapeDtypeStruct((shard, hid), F32)...]
where the time goes in v2:
time: 187 us
  Pallas kernels  179 us (96%)
  local copies, waits for them, and re-layouts  6.83 us (4%)
    pallas_call x1, Pallas kernels, on_device(): pl.pallas_call(kernel, out_shape=(jax.ShapeDtypeStruct((shard, hid), F32)...  179 us
    unnamed x5, local copies, waits for them, and re-layouts  5.55 us

profile of v2, /device:TPU:1, one launch (start us, length us, event | category | flops | bytes accessed | tf_op | source)
XLA Modules:
  0.0 186.7 jit_solution(442491413581966471)
XLA Ops:
  0.6 2.0 %copy.7 = bf16[1,1024,256]{1,2,0:T(8,128)(2,1)} copy(bf16[1,1024,256]{2,1,0:T(8,128)(2,1)} %param.6) | data formatting | bytes 1048576 | tf_op args[2]
  2.7 179.3 %shard_map.67 = (f32[256,1024]{1,0:T(8,128)}, f32[256,1024]{1,0:T(8,128)}, f32[8,128]{1,0:T(8,128)}) custom-call(bf16[2,128,4096]{2,1,0:T(8,128)(2,1)} %x_hbm.1, bf16[256,1024]{1,0:T(8,128)(2,1)} %bitcast.12, bf16[256,1024]{1,0:T(8,128)(2,1)} %bitcast.9, bf16[2,128,4096]{2,1,0:T(8,128)(2,1)} %cot_hbm.1), custom_call_target="tpu_custom_call" | custom-call | tf_op jit(solution)/shard_map/pallas_call | solution.py:483
  181.9 0.0 copy-start
  181.9 1.3 slice.3
  183.2 2.5 %copy.8 = f32[1,1024,256]{2,1,0:T(8,128)} copy(f32[1,1024,256]{1,2,0:T(8,128)} %bitcast.11) | data formatting | bytes 2097152
  185.8 0.0 copy-done
  185.8 1.0 copy.10
Async XLA Ops:
  181.9 3.8 %copy-start = (f32[256,1024]{1,0:T(8,128)S(1)}, f32[256,1024]{1,0:T(8,128)}, u32[]{:S(2)}) copy-start(f32[256,1024]{1,0:T(8,128)} %get-tuple-element.6) | copy-start | bytes 3145732

commit v3 on v0

v3 whole, which is shorter than its diff:
```python
import jax
import jax.numpy as jnp
from jax import lax
from jax.experimental import pallas as pl
from jax.experimental.pallas import tpu as pltpu
from jax.sharding import Mesh
from jax.sharding import PartitionSpec as P

CLIP_NORM = 16384.0
AXES = ("pipe", "xhi", "core", "z", "y")
TENSOR = ("xhi", "core")
DP = ("z", "y")
PIPE_TENSOR_DP = ("pipe", "xhi", "core", "z", "y")
TENSOR_DP = ("xhi", "core", "z", "y")
MESH = pl.DeviceIdType.MESH
BF = jnp.bfloat16
F32 = jnp.float32

RING = 4
NT = (((1,), (1,)), ((), ()))
TN = (((0,), (0,)), ((), ()))


def kernel(
    x_hbm, win_hbm, wot_hbm, cot_hbm,
    upd_in, upd_out, norm_out,
    stage, x0, cot, x1, err1, own, w, g, act, slope,
    part, r1, r2, keep,
    rc, ra, rb,
    fin, pex, prx, nsum, n1, n2,
    lsem, ssem, rsem,
):
    group, hid = part.shape[2], part.shape[3]
    rows = RING * group
    sub = w.shape[3]
    hl = hid // 2
    chunk = group // RING
    hs = sub // 2
    part_d = x0.shape[-1]
    tile = 256
    pipe = lax.axis_index("pipe")
    xhi = lax.axis_index("xhi")
    core = lax.axis_index("core")
    z = lax.axis_index("z")
    y = lax.axis_index("y")
    other = 1 - pipe
    core2 = 1 - core
    xi = xhi * 2 + pipe

    def turn(v, d):
        return lax.rem(v + d, RING)

    started = []
    count = [0]
    lcount = [0]

    def remote(src, dst, dev):
        i = count[0]
        count[0] += 1
        copy = pltpu.make_async_remote_copy(
            src_ref=src, dst_ref=dst, send_sem=ssem.at[i], recv_sem=rsem.at[i],
            device_id=dev, device_id_type=MESH,
        )
        copy.start()
        started.append(copy)
        return copy

    def same(ref, dev):
        return remote(ref, ref, dev)

    def local(src, dst):
        i = lcount[0]
        lcount[0] += 1
        copy = pltpu.make_async_copy(src, dst, lsem.at[i])
        copy.start()
        return copy

    def wait_all(copies):
        for copy in copies:
            copy.wait_recv()

    xpeers = []
    for code in (3, 2, 1):
        p_ = other if code % 2 else pipe
        h_ = 1 - xhi if code // 2 else xhi
        xpeers.append((code, {"pipe": p_, "xhi": h_}, h_ * 2 + p_))
    ypeers = [(d, {"y": turn(y, d)}, turn(y, d)) for d in (2, 1, 3)]
    zpeers = [(d, {"z": turn(z, d)}) for d in (1, 2, 3)]
    up, dn = {"z": turn(z, 1)}, {"z": turn(z, 3)}
    zu, zd, z2 = turn(z, 1), turn(z, 3), turn(z, 2)
    twin = {"core": core2}
    pair = {"pipe": other}
    ycore = [(d * 2, {**dev}, yy, core) for d, dev, yy in ypeers]
    ycore += [(d * 2 + 1, {**dev, "core": core2}, yy, core2) for d, dev, yy in ypeers]
    ycore += [(1, twin, y, core2)]
    xz = [(code, dev) for code, dev, _ in xpeers]
    xz += [(d * 4, dev) for d, dev in zpeers]
    xz += [(d * 4 + code, {**dx, **dz}) for d, dz in zpeers for code, dx, _ in xpeers]

    keep_rows = pl.ds(pl.multiple_of(pipe * sub, sub), sub)
    give_rows = pl.ds(pl.multiple_of(other * sub, sub), sub)
    own_load = [
        local(win_hbm.at[give_rows, :], own.at[0]),
        local(wot_hbm.at[give_rows, :], own.at[1]),
        local(win_hbm.at[keep_rows, :], w.at[2 * pipe, core, z]),
        local(wot_hbm.at[keep_rows, :], w.at[2 * pipe + 1, core, z]),
    ]

    def fetch(src, n):
        copies = []
        for yy in range(RING):
            for zz in range(RING):
                off = pl.multiple_of((zz * RING + yy) * 2 * sub + pipe * sub, sub)
                copies.append(
                    local(src.at[:, :, pl.ds(off, sub)], stage.at[n, yy, :, :, pl.ds(zz * sub, sub)])
                )
        return copies

    x_load = fetch(x_hbm, 0)
    cot_load = fetch(cot_hbm, 1)

    barrier = pltpu.get_barrier_semaphore()
    peers = [dev for _, dev, _, _ in ycore] + [dev for _, dev in xz]
    for dev in peers:
        pl.semaphore_signal(barrier, inc=1, device_id=dev, device_id_type=MESH)
    pl.semaphore_wait(barrier, len(peers))

    half_tok = x0.shape[2]
    my_cols = pl.ds(pl.multiple_of(core * (part_d // 2), part_d // 2), part_d // 2)

    def swap_tokens(n, dst):
        def piece(yy, cc):
            toks = pl.ds(pl.multiple_of(cc * half_tok, half_tok), half_tok)
            return stage.at[n, yy, :, toks, :]

        landing = dst.at[y, :, :, my_cols]
        return local(piece(y, core), landing), [
            remote(piece(yy, cc), landing, dev) for _, dev, yy, cc in ycore
        ]

    lo, hi = pl.ds(0, hs), pl.ds(hs, hs)

    def g1(k):
        ref = w.at[k, core, z]
        return [same(ref, up), same(ref, dn)]

    def g2(k):
        ring = [same(w.at[k, core, zd, lo, :], up), same(w.at[k, core, zu, hi, :], dn)]
        return ring, [same(w.at[k, core, at], twin) for at in (z, zu, zd)]

    def g3(k):
        return [same(w.at[k, core, z2], twin)]

    halves = (pl.ds(0, hl), pl.ds(hl, hl))

    def project(src, k, ph, half):
        @pl.loop(0, hl // tile)
        def _(n):
            cols = pl.ds(pl.multiple_of(half * hl + n * tile, tile), tile)
            left = src[...].reshape(rows, part_d)
            right = w[k, :, :, :, cols].reshape(part_d, tile)
            got = jnp.dot(left, right, preferred_element_type=F32)
            part[ph, :, :, cols] = got.astype(BF).reshape(RING, group, tile)

    def widen(base, units, k, out):
        for cc in range(2):
            @pl.loop(0, 2)
            def _(p):
                cols = pl.ds(pl.multiple_of(cc * RING * sub + p * 2 * sub, tile), 2 * sub)
                left = units[...].reshape(rows, hid)
                right = w[k, cc, pl.ds(p * 2, 2)].reshape(2 * sub, hid)
                add = lax.dot_general(left, right, NT, preferred_element_type=F32)
                old = base[:, :, :, cols].reshape(rows, 2 * sub).astype(F32)
                out[:, :, :, cols] = (old + add).astype(BF).reshape(RING, 2, half_tok, 2 * sub)

    def weight_grad(left_ref, right, k):
        def side(cc):
            @pl.loop(0, 2)
            def _(p):
                cols = pl.ds(pl.multiple_of(cc * RING * sub + p * 2 * sub, tile), 2 * sub)
                left = left_ref[:, :, :, cols].reshape(rows, 2 * sub)
                units = right[...].reshape(rows, hid)
                got = lax.dot_general(left, units, TN, preferred_element_type=F32)
                g[k, cc, pl.ds(p * 2, 2)] = got.astype(BF).reshape(2, sub, hid)

        side(core2)
        copy = remote(g.at[k, core2], rc.at[k], twin)
        side(core)
        return [copy]

    def plus(x, *more):
        total = x.astype(F32)
        for m in more:
            total = total + m.astype(F32)
        return total

    first = (xpeers, ypeers)
    second = (ypeers, xpeers)
    block = (xi, y)
    inner = (y, xi)

    def inner_rows(at):
        return pl.ds(pl.multiple_of(at * chunk, chunk), chunk)

    def rs1(ph, half):
        lanes = halves[half]
        return [
            remote(part.at[ph, at, :, lanes], r1.at[ph, half, slot], dev)
            for slot, dev, at in first[half]
        ]

    def rs2(ph, half, copies):
        wait_all(copies)
        lanes = halves[half]
        b = block[half]
        part[ph, b, :, lanes] = plus(
            part[ph, b, :, lanes], r1[ph, half, 1], r1[ph, half, 2], r1[ph, half, 3]
        ).astype(BF)
        return [
            remote(part.at[ph, b, inner_rows(at), lanes], r2.at[ph, half, slot], dev)
            for slot, dev, at in second[half]
        ]

    def units(ph, half, copies):
        wait_all(copies)
        return plus(
            part[ph, block[half], inner_rows(inner[half]), halves[half]],
            r2[ph, half, 1], r2[ph, half, 2], r2[ph, half, 3],
        )

    def sp1(ref, half, value):
        b, at, lanes = block[half], inner_rows(inner[half]), halves[half]
        ref[b, at, lanes] = value
        piece = ref.at[b, at, lanes]
        return [same(piece, dev) for _, dev, _ in second[half]]

    def sp2(ref, half, copies):
        wait_all(copies)
        piece = ref.at[block[half], :, halves[half]]
        return [same(piece, dev) for _, dev, _ in first[half]]

    def slope_of(upward, pre):
        sig = jax.nn.sigmoid(pre)
        return (upward * sig * (1.0 + pre * (1.0 - sig))).astype(BF)

    def q1(k, copies):
        wait_all(copies)
        g[k, core, z2] = plus(g[k, core, z2], rc[k, z2]).astype(BF)
        return [
            remote(g.at[k, core, z2, lo, :], ra.at[k, 0], up),
            remote(g.at[k, core, z2, hi, :], ra.at[k, 1], dn),
        ]

    def q2(k, copies):
        g[k, core, zu, hi, :] = plus(g[k, core, zu, hi, :], rc[k, zu, hi, :]).astype(BF)
        g[k, core, zd, lo, :] = plus(g[k, core, zd, lo, :], rc[k, zd, lo, :]).astype(BF)
        wait_all(copies)
        g[k, core, zu, lo, :] = plus(g[k, core, zu, lo, :], rc[k, zu, lo, :], ra[k, 0]).astype(BF)
        g[k, core, zd, hi, :] = plus(g[k, core, zd, hi, :], rc[k, zd, hi, :], ra[k, 1]).astype(BF)
        return [
            remote(g.at[k, core, zu], rb.at[k, 0], up),
            remote(g.at[k, core, zd], rb.at[k, 1], dn),
        ]

    def fold(value):
        lanes = value.shape[-1]
        value = value.reshape(sub // 8, 8, lanes).sum(0)
        total = value[:, 0:128]
        for i in range(1, lanes // 128):
            total = total + value[:, i * 128 : (i + 1) * 128]
        return total

    def finish(k, copies):
        wait_all(copies)
        value = plus(g[k, core, z], rc[k, z], rb[k, 0], rb[k, 1])
        fin[k] = value
        return fold(value * value)

    def hand_over(kind):
        pex[kind] = fin[2 * other + kind].astype(BF)
        return remote(pex.at[kind], prx.at[kind], pair)

    for copy in own_load:
        copy.wait()
    k_own = (3 * pipe, 1 + pipe)
    k_got = (3 * other, 1 + other)
    ca0 = g1(k_own[0])
    e0 = remote(own.at[pipe], w.at[3 * pipe, core, z], pair)
    e1 = remote(own.at[other], w.at[1 + pipe, core, z], pair)
    for copy in x_load:
        copy.wait()
    x_here, x_swap = swap_tokens(0, x0)
    e0.wait_recv()
    ca1 = g1(k_got[0])
    wait_all(ca0)
    cb0, cc0 = g2(k_own[0])
    for copy in cot_load:
        copy.wait()
    cot_here, cot_swap = swap_tokens(1, cot)
    wait_all(ca1)
    cb1, cc1 = g2(k_got[0])
    ca2 = g1(k_own[1])
    e1.wait_recv()
    ca3 = g1(k_got[1])
    wait_all(cb0)
    cd0 = g3(k_own[0])
    wait_all(cb1)
    cd1 = g3(k_got[0])
    x_here.wait()
    wait_all(x_swap)
    wait_all(cc0 + cc1)
    wait_all(cd0 + cd1)
    project(x0, 0, 0, 0)
    p0a = rs1(0, 0)
    project(x0, 0, 0, 1)
    p0b = rs1(0, 1)
    wait_all(ca2)
    cb2, cc2 = g2(k_own[1])
    wait_all(ca3)
    cb3, cc3 = g2(k_got[1])
    cot_here.wait()
    wait_all(cot_swap)
    project(cot, 3, 2, 0)
    project(cot, 3, 2, 1)
    p0a = rs2(0, 0, p0a)
    p0b = rs2(0, 1, p0b)
    wait_all(cb2)
    cd2 = g3(k_own[1])
    pre = units(0, 0, p0a)
    keep[0, 0] = pre
    a0a = sp1(act.at[0], 0, jax.nn.silu(pre).astype(BF))
    pre = units(0, 1, p0b)
    keep[0, 1] = pre
    a0b = sp1(act.at[0], 1, jax.nn.silu(pre).astype(BF))
    a0a = sp2(act.at[0], 0, a0a)
    a0b = sp2(act.at[0], 1, a0b)
    p2a = rs1(2, 0)
    p2b = rs1(2, 1)
    wait_all(cb3)
    cd3 = g3(k_got[1])
    wait_all(cc2 + cc3)
    wait_all(cd2 + cd3)
    wait_all(a0a)
    wait_all(a0b)
    widen(x0, act.at[0], 1, x1)
    project(x1, 2, 1, 0)
    p1a = rs1(1, 0)
    project(x1, 2, 1, 1)
    p1b = rs1(1, 1)
    p2a = rs2(2, 0, p2a)
    p2b = rs2(2, 1, p2b)
    up1a = units(2, 0, p2a)
    keep[1, 0] = up1a
    up1b = units(2, 1, p2b)
    keep[1, 1] = up1b
    p1a = rs2(1, 0, p1a)
    p1b = rs2(1, 1, p1b)
    pre = units(1, 0, p1a)
    s1a = sp1(slope.at[1], 0, slope_of(keep[1, 0], pre))
    a1a = sp1(act.at[1], 0, jax.nn.silu(pre).astype(BF))
    pre = units(1, 1, p1b)
    s1b = sp1(slope.at[1], 1, slope_of(keep[1, 1], pre))
    a1b = sp1(act.at[1], 1, jax.nn.silu(pre).astype(BF))
    s1a = sp2(slope.at[1], 0, s1a)
    s1b = sp2(slope.at[1], 1, s1b)
    a1a = sp2(act.at[1], 0, a1a)
    a1b = sp2(act.at[1], 1, a1b)
    wait_all(s1a)
    wait_all(s1b)
    widen(cot, slope.at[1], 2, err1)
    project(err1, 1, 3, 0)
    p3a = rs1(3, 0)
    project(err1, 1, 3, 1)
    p3b = rs1(3, 1)
    d2 = weight_grad(x1, slope.at[1], 2)
    d1 = weight_grad(err1, act.at[0], 1)
    d2 = q1(2, d2)
    p3a = rs2(3, 0, p3a)
    p3b = rs2(3, 1, p3b)
    d1 = q1(1, d1)
    d2 = q2(2, d2)
    s0a = sp1(slope.at[0], 0, slope_of(units(3, 0, p3a), keep[0, 0]))
    s0b = sp1(slope.at[0], 1, slope_of(units(3, 1, p3b), keep[0, 1]))
    wait_all(a1a)
    wait_all(a1b)
    d3 = weight_grad(cot, act.at[1], 3)
    s0a = sp2(slope.at[0], 0, s0a)
    s0b = sp2(slope.at[0], 1, s0b)
    d3 = q1(3, d3)
    d1 = q2(1, d1)
    squares = finish(2, d2)
    wait_all(s0a)
    wait_all(s0b)
    d0 = weight_grad(x0, slope.at[0], 0)
    d0 = q1(0, d0)
    d3 = q2(3, d3)
    squares = squares + finish(1, d1)
    d0 = q2(0, d0)
    squares = squares + finish(3, d3)
    h1 = hand_over(1)
    squares = squares + finish(0, d0)
    nsum[0] = squares
    c1 = [remote(nsum.at[0], n1.at[code], dev) for code, dev, _, _ in ycore]
    h0 = hand_over(0)
    wait_all(c1)
    total = nsum[0]
    for code in range(1, 8):
        total = total + n1[code]
    nsum[1] = total
    c2 = [remote(nsum.at[1], n2.at[code], dev) for code, dev in xz]
    wait_all(c2)
    total = nsum[1]
    for code in range(1, 16):
        total = total + n2[code]
    norm = jnp.sqrt(jnp.sum(total, keepdims=True))
    norm_out[...] = jnp.broadcast_to(norm, norm_out.shape)
    factor = jnp.minimum(1.0, CLIP_NORM / norm)
    h1.wait_recv()
    h0.wait_recv()
    for kind, out in ((0, upd_in), (1, upd_out)):
        out[keep_rows, :] = fin[2 * pipe + kind] * factor
        out[give_rows, :] = prx[kind].astype(F32) * factor
    for copy in started:
        copy.wait_send()


def on_device(inputs, w_in, w_out, cotangent):
    micro, tok, cols = inputs.shape
    shard, hid = w_in.shape[1], w_in.shape[2]
    sub = shard // 2
    part_d = cols // 4
    group = micro * tok // 2
    hl = hid // 2
    any_spec = pl.BlockSpec(memory_space=pl.ANY)
    vmem = pl.BlockSpec(memory_space=pltpu.VMEM)
    tokens = pltpu.VMEM((RING, micro, tok // 2, part_d), BF)
    weights = pltpu.VMEM((4, 2, RING, sub, hid), BF)
    layers = pltpu.VMEM((2, RING, group, hid), BF)
    upd_in, upd_out_t, norm = pl.pallas_call(
        kernel,
        out_shape=(
            jax.ShapeDtypeStruct((shard, hid), F32),
            jax.ShapeDtypeStruct((shard, hid), F32),
            jax.ShapeDtypeStruct((8, 128), F32),
        ),
        in_specs=[any_spec] * 4,
        out_specs=(vmem, vmem, vmem),
        scratch_shapes=[
            pltpu.VMEM((2, RING, micro, tok, RING * sub), BF),
            tokens, tokens, tokens, tokens,
            pltpu.VMEM((2, sub, hid), BF),
            weights, weights, layers, layers,
            pltpu.VMEM((4, RING, group, hid), BF),
            pltpu.VMEM((4, 2, RING, group, hl), BF),
            pltpu.VMEM((4, 2, RING, group // RING, hl), BF),
            pltpu.VMEM((2, 2, group // RING, hl), F32),
            pltpu.VMEM((4, RING, sub, hid), BF),
            pltpu.VMEM((4, 2, sub // 2, hid), BF),
            pltpu.VMEM((4, 2, sub, hid), BF),
            pltpu.VMEM((4, sub, hid), F32),
            pltpu.VMEM((2, sub, hid), BF),
            pltpu.VMEM((2, sub, hid), BF),
            pltpu.VMEM((2, 8, 128), F32),
            pltpu.VMEM((8, 8, 128), F32),
            pltpu.VMEM((16, 8, 128), F32),
            pltpu.SemaphoreType.DMA((40,)),
            pltpu.SemaphoreType.DMA((200,)),
            pltpu.SemaphoreType.DMA((200,)),
        ],
        compiler_params=pltpu.CompilerParams(
            collective_id=0, has_side_effects=True, vmem_limit_bytes=67043328
        ),
    )(inputs, w_in[0], w_out[0].T, cotangent)
    return upd_in[None], upd_out_t.T[None], norm[0, 0]


def solution(mesh):
    split = Mesh(mesh.devices.reshape(mesh.shape["pipe"], 2, 2, RING, RING), AXES)
    placed = (
        P(None, DP, TENSOR),
        P("pipe", TENSOR_DP, None),
        P("pipe", None, TENSOR_DP),
        P(None, DP, TENSOR),
    )
    return jax.shard_map(
        on_device,
        mesh=split,
        in_specs=placed,
        out_specs=(P("pipe", TENSOR_DP, None), P("pipe", None, TENSOR_DP), P()),
        check_vma=False,
    )
```

time: 890 us -> 156 us (0.18)
  waiting for transfers between devices: 598 us -> 0 us
  Pallas kernels: 0 us -> 148 us
  matrix products: 90.1 us -> 0 us
  other arithmetic: 62.4 us -> 0 us
  local copies, waits for them, and re-layouts: 66.9 us -> 6.83 us
  blocking collectives: 32.1 us -> 0 us
  between operations: 17 us -> 0.65 us
  starting transfers between devices: 14.4 us -> 0 us
    all_gather x7 -> x0, waiting for transfers between devices: 293 us -> none  [the longest x6 178 us: total_of_pieces(): return lax.all_gather(value, axis).sum(0)]
    reduce_scatter x2 -> x0, waiting for transfers between devices: 208 us -> none  [the longest x1 111 us: on_device(): lax.psum_scatter(total_in, DP, scatter_dimension=0, tiled=True)]
    pallas_call x0 -> x1, Pallas kernels: none -> 148 us  [on_device(): pl.pallas_call(kernel, out_shape=(jax.ShapeDtypeStruct((shard, hid), F32)...]
    ppermute x6 -> x0, waiting for transfers between devices: 96.7 us -> none  [from_behind(): return lax.ppermute(value, axis, pairs)]
    dot_general x12 -> x0, matrix products: 90.1 us -> none  [the longest x2 25.8 us: accumulate(): jnp.einsum('gtc,gth->gch', x_groups, slope_groups, preferred_element_type...]
    reduce_sum x10 -> x0, other arithmetic: 40.4 us -> none  [the longest x1 13.2 us: on_device(): jnp.sum(sum_in.astype(jnp.float32) - err_in.astype(jnp.float32), axis=0)]
    psum x5 -> x0, blocking collectives: 32.1 us -> none  [by_axis(): value = lax.psum(value, axis)]
    while x31 -> x0, local copies, waits for them, and re-layouts: 21.9 us -> none  [the longest x1 11.3 us: on_device(): lax.scan(backward_step, (zero_rows, sums_init), jnp.arange(step_count))]
  transfers between devices with their start and end apart: 15 -> 0, of which waited for: 13 -> 0; matrix products, arithmetic and copies ran while one was open for 7% -> 0% of each run, Pallas kernels for 0% -> 0%
where the time goes in v3:
time: 156 us
  Pallas kernels  148 us (95%)
  local copies, waits for them, and re-layouts  6.83 us (4%)
    pallas_call x1, Pallas kernels, on_device(): pl.pallas_call(kernel, out_shape=(jax.ShapeDtypeStruct((shard, hid), F32)...  148 us
    unnamed x5, local copies, waits for them, and re-layouts  5.55 us

profile of v3, /device:TPU:1, one launch (start us, length us, event | category | flops | bytes accessed | tf_op | source)
XLA Modules:
  0.0 155.8 jit_solution(6122809190505756437)
XLA Ops:
  0.6 2.0 %copy.7 = bf16[1,1024,256]{1,2,0:T(8,128)(2,1)} copy(bf16[1,1024,256]{2,1,0:T(8,128)(2,1)} %param.6) | data formatting | bytes 1048576 | tf_op args[2]
  2.7 148.3 %shard_map.67 = (f32[256,1024]{1,0:T(8,128)}, f32[256,1024]{1,0:T(8,128)}, f32[8,128]{1,0:T(8,128)}) custom-call(bf16[2,128,4096]{2,1,0:T(8,128)(2,1)} %x_hbm.1, bf16[256,1024]{1,0:T(8,128)(2,1)} %bitcast.12, bf16[256,1024]{1,0:T(8,128)(2,1)} %bitcast.9, bf16[2,128,4096]{2,1,0:T(8,128)(2,1)} %cot_hbm.1), custom_call_target="tpu_custom_call" | custom-call | tf_op jit(solution)/shard_map/pallas_call | solution.py:439
  151.0 0.0 copy-start
  151.0 1.3 slice.3
  152.3 2.5 %copy.8 = f32[1,1024,256]{2,1,0:T(8,128)} copy(f32[1,1024,256]{1,2,0:T(8,128)} %bitcast.11) | data formatting | bytes 2097152
  154.8 0.0 copy-done
  154.8 1.0 copy.10
Async XLA Ops:
  151.0 3.8 %copy-start = (f32[256,1024]{1,0:T(8,128)S(1)}, f32[256,1024]{1,0:T(8,128)}, u32[]{:S(2)}) copy-start(f32[256,1024]{1,0:T(8,128)} %get-tuple-element.6) | copy-start | bytes 3145732

commit v4 on v3

v4 whole, which is shorter than its diff:
```python
import jax
import jax.numpy as jnp
from jax import lax
from jax.experimental import pallas as pl
from jax.experimental.pallas import tpu as pltpu
from jax.sharding import Mesh
from jax.sharding import PartitionSpec as P

CLIP_NORM = 16384.0
AXES = ("pipe", "xhi", "core", "z", "y")
TENSOR = ("xhi", "core")
DP = ("z", "y")
PIPE_TENSOR_DP = ("pipe", "xhi", "core", "z", "y")
TENSOR_DP = ("xhi", "core", "z", "y")
MESH = pl.DeviceIdType.MESH
BF = jnp.bfloat16
F32 = jnp.float32

RING = 4
NT = (((1,), (1,)), ((), ()))
TN = (((0,), (0,)), ((), ()))


def kernel(
    x_hbm, win_hbm, wout_hbm, cot_hbm,
    tot_in, tot_out, norm_out,
    stage, x0, cot, x1, err1, raw, own, w, g, act, slope,
    part, r1, r2, keep,
    rc, ra, rb,
    fin, pex, prx, late, turned, nsum, n1, n2,
    lsem, ssem, rsem,
):
    group, hid = part.shape[2], part.shape[3]
    rows = RING * group
    sub = w.shape[3]
    hl = hid // 2
    hs = sub // 2
    part_d = x0.shape[-1]
    tile = 256
    pipe = lax.axis_index("pipe")
    xhi = lax.axis_index("xhi")
    core = lax.axis_index("core")
    z = lax.axis_index("z")
    y = lax.axis_index("y")
    other = 1 - pipe
    core2 = 1 - core
    xi = xhi * 2 + pipe

    def turn(v, d):
        return lax.rem(v + d, RING)

    started = []
    count = [0]
    lcount = [0]

    def remote(src, dst, dev):
        i = count[0]
        count[0] += 1
        copy = pltpu.make_async_remote_copy(
            src_ref=src, dst_ref=dst, send_sem=ssem.at[i], recv_sem=rsem.at[i],
            device_id=dev, device_id_type=MESH,
        )
        copy.start()
        started.append(copy)
        return copy

    def same(ref, dev):
        return remote(ref, ref, dev)

    def local(src, dst):
        i = lcount[0]
        lcount[0] += 1
        copy = pltpu.make_async_copy(src, dst, lsem.at[i])
        copy.start()
        return copy

    def wait_all(copies):
        for copy in copies:
            copy.wait_recv()

    xpeers = []
    for code in (3, 2, 1):
        p_ = other if code % 2 else pipe
        h_ = 1 - xhi if code // 2 else xhi
        xpeers.append((code, {"pipe": p_, "xhi": h_}, h_ * 2 + p_))
    ypeers = [(d, {"y": turn(y, d)}, turn(y, d)) for d in (2, 1, 3)]
    zpeers = [(d, {"z": turn(z, d)}) for d in (1, 2, 3)]
    up, dn = {"z": turn(z, 1)}, {"z": turn(z, 3)}
    zu, zd, z2 = turn(z, 1), turn(z, 3), turn(z, 2)
    twin = {"core": core2}
    pair = {"pipe": other}
    ycore = [(d * 2, {**dev}, yy, core) for d, dev, yy in ypeers]
    ycore += [(d * 2 + 1, {**dev, "core": core2}, yy, core2) for d, dev, yy in ypeers]
    ycore += [(1, twin, y, core2)]
    xz = [(code, dev) for code, dev, _ in xpeers]
    xz += [(d * 4, dev) for d, dev in zpeers]
    xz += [(d * 4 + code, {**dx, **dz}) for d, dz in zpeers for code, dx, _ in xpeers]

    keep_rows = pl.ds(pl.multiple_of(pipe * sub, sub), sub)
    give_rows = pl.ds(pl.multiple_of(other * sub, sub), sub)
    out_load = [
        local(wout_hbm.at[:, give_rows], raw.at[0]),
        local(wout_hbm.at[:, keep_rows], raw.at[1]),
    ]
    own_load = [
        local(win_hbm.at[give_rows, :], own.at[0]),
        local(win_hbm.at[keep_rows, :], w.at[2 * pipe, core, z]),
    ]

    def fetch(src, n):
        copies = []
        for yy in range(RING):
            for zz in range(RING):
                off = pl.multiple_of((zz * RING + yy) * 2 * sub + pipe * sub, sub)
                copies.append(
                    local(src.at[:, :, pl.ds(off, sub)], stage.at[n, yy, :, :, pl.ds(zz * sub, sub)])
                )
        return copies

    x_load = fetch(x_hbm, 0)
    cot_load = fetch(cot_hbm, 1)

    barrier = pltpu.get_barrier_semaphore()
    peers = [dev for _, dev, _, _ in ycore] + [dev for _, dev in xz]
    for dev in peers:
        pl.semaphore_signal(barrier, inc=1, device_id=dev, device_id_type=MESH)
    for copy in out_load:
        copy.wait()
    own[1] = raw[0].T
    w[2 * pipe + 1, core, z] = raw[1].T
    pl.semaphore_wait(barrier, len(peers))

    half_tok = x0.shape[2]
    my_cols = pl.ds(pl.multiple_of(core * (part_d // 2), part_d // 2), part_d // 2)

    def swap_tokens(n, dst):
        def piece(yy, cc):
            toks = pl.ds(pl.multiple_of(cc * half_tok, half_tok), half_tok)
            return stage.at[n, yy, :, toks, :]

        landing = dst.at[y, :, :, my_cols]
        return local(piece(y, core), landing), [
            remote(piece(yy, cc), landing, dev) for _, dev, yy, cc in ycore
        ]

    lo, hi = pl.ds(0, hs), pl.ds(hs, hs)

    def g1(k, rows_of=slice(None)):
        ref = w.at[k, core, z, rows_of, :]
        return [same(ref, up), same(ref, dn)]

    def g2(k, cuts=(lo, hi)):
        ring = [same(w.at[k, core, zd, r, :], up) for r in cuts[: len(cuts) // 2]]
        ring += [same(w.at[k, core, zu, r, :], dn) for r in cuts[len(cuts) // 2 :]]
        return ring

    def g2c(k):
        return [same(w.at[k, core, at], twin) for at in (z, zu, zd)]

    def g3(k):
        return [same(w.at[k, core, z2], twin)]

    halves = (pl.ds(0, hl), pl.ds(hl, hl))

    mrows = group // 2
    streams = (pl.ds(0, mrows), pl.ds(mrows, mrows))
    srows = RING * mrows

    def project(src, k, ph, half, m):
        @pl.loop(0, hl // tile)
        def _(n):
            cols = pl.ds(pl.multiple_of(half * hl + n * tile, tile), tile)
            left = src[:, m].reshape(srows, part_d)
            right = w[k, :, :, :, cols].reshape(part_d, tile)
            got = jnp.dot(left, right, preferred_element_type=F32)
            part[ph, :, streams[m], cols] = got.astype(BF).reshape(RING, mrows, tile)

    def widen(base, units_ref, k, out, m):
        for cc in range(2):
            @pl.loop(0, 2)
            def _(p):
                cols = pl.ds(pl.multiple_of(cc * RING * sub + p * 2 * sub, tile), 2 * sub)
                left = units_ref[:, streams[m], :].reshape(srows, hid)
                right = w[k, cc, pl.ds(p * 2, 2)].reshape(2 * sub, hid)
                add = lax.dot_general(left, right, NT, preferred_element_type=F32)
                old = base[:, m, :, cols].reshape(srows, 2 * sub).astype(F32)
                out[:, m, :, cols] = (old + add).astype(BF).reshape(RING, mrows, 2 * sub)

    def weight_grad(left_ref, right, k):
        def side(cc, p):
            zz = pl.ds(pl.multiple_of(p * 2, 2), 2)
            cols = pl.ds(pl.multiple_of(cc * RING * sub + p * 2 * sub, tile), 2 * sub)
            left = left_ref[:, :, :, cols].reshape(rows, 2 * sub)
            got = lax.dot_general(left, right[...].reshape(rows, hid), TN, preferred_element_type=F32)
            g[k, cc, zz] = got.astype(BF).reshape(2, sub, hid)

        def across(p):
            zz = pl.ds(pl.multiple_of(p * 2, 2), 2)
            return remote(g.at[k, core2, zz], rc.at[k, zz], twin)

        p_far = z2 // 2
        p_near = 1 - p_far
        side(core2, p_far)
        far = across(p_far)
        side(core2, p_near)
        near = across(p_near)
        side(core, p_far)
        sent = q1(k, [far])
        side(core, p_near)
        return sent, near

    def plus(x, *more):
        total = x.astype(F32)
        for m in more:
            total = total + m.astype(F32)
        return total

    first = (xpeers, ypeers)
    second = (ypeers, xpeers)
    block = (xi, y)
    inner = (y, xi)

    crows = mrows // RING

    def inner_rows(at, m):
        return pl.ds(pl.multiple_of(m * mrows + at * crows, crows), crows)

    def slots(m):
        return pl.ds(m * crows, crows)

    def rs1(ph, half, m):
        lanes, r = halves[half], streams[m]
        return [
            remote(part.at[ph, at, r, lanes], r1.at[ph, half, slot, r], dev)
            for slot, dev, at in first[half]
        ]

    def rs2(ph, half, m, copies):
        wait_all(copies)
        lanes, r = halves[half], streams[m]
        b = block[half]
        part[ph, b, r, lanes] = plus(
            part[ph, b, r, lanes], r1[ph, half, 1, r], r1[ph, half, 2, r], r1[ph, half, 3, r]
        ).astype(BF)
        return [
            remote(part.at[ph, b, inner_rows(at, m), lanes], r2.at[ph, half, slot, slots(m)], dev)
            for slot, dev, at in second[half]
        ]

    def units(ph, half, m, copies):
        wait_all(copies)
        c = slots(m)
        return plus(
            part[ph, block[half], inner_rows(inner[half], m), halves[half]],
            r2[ph, half, 1, c], r2[ph, half, 2, c], r2[ph, half, 3, c],
        )

    def put(ref, half, m, value):
        ref[block[half], inner_rows(inner[half], m), halves[half]] = value

    def sp1(ref, half, m):
        piece = ref.at[block[half], inner_rows(inner[half], m), halves[half]]
        return [same(piece, dev) for _, dev, _ in second[half]]

    def sp2(ref, half, m, copies):
        wait_all(copies)
        piece = ref.at[block[half], streams[m], halves[half]]
        return [same(piece, dev) for _, dev, _ in first[half]]

    def slope_of(upward, pre):
        sig = jax.nn.sigmoid(pre)
        return (upward * sig * (1.0 + pre * (1.0 - sig))).astype(BF)

    def q1(k, copies):
        wait_all(copies)
        g[k, core, z2] = plus(g[k, core, z2], rc[k, z2]).astype(BF)
        return [
            remote(g.at[k, core, z2, lo, :], ra.at[k, 0], up),
            remote(g.at[k, core, z2, hi, :], ra.at[k, 1], dn),
        ]

    def q2(k, copies, near):
        near.wait_recv()
        g[k, core, zu, hi, :] = plus(g[k, core, zu, hi, :], rc[k, zu, hi, :]).astype(BF)
        g[k, core, zd, lo, :] = plus(g[k, core, zd, lo, :], rc[k, zd, lo, :]).astype(BF)
        wait_all(copies)
        g[k, core, zu, lo, :] = plus(g[k, core, zu, lo, :], rc[k, zu, lo, :], ra[k, 0]).astype(BF)
        g[k, core, zd, hi, :] = plus(g[k, core, zd, hi, :], rc[k, zd, hi, :], ra[k, 1]).astype(BF)
        return [
            remote(g.at[k, core, zu], rb.at[k, 0], up),
            remote(g.at[k, core, zd], rb.at[k, 1], dn),
        ]

    def fold(value):
        lanes = value.shape[-1]
        value = value.reshape(sub // 8, 8, lanes).sum(0)
        total = value[:, 0:128]
        for i in range(1, lanes // 128):
            total = total + value[:, i * 128 : (i + 1) * 128]
        return total

    def finish(k, copies):
        wait_all(copies)
        value = plus(g[k, core, z], rc[k, z], rb[k, 0], rb[k, 1])
        fin[k] = value
        return fold(value * value)

    def hand_over(kind):
        pex[kind] = fin[2 * other + kind].astype(BF)
        return remote(pex.at[kind], prx.at[kind], pair)

    HALVES = (0, 1)

    def both(f):
        return [f(half) for half in HALVES]

    def project_send(src, k, ph, m):
        sent = []
        for half in HALVES:
            project(src, k, ph, half, m)
            sent.append(rs1(ph, half, m))
        return sent

    def all_rs2(ph, m, sent):
        return both(lambda half: rs2(ph, half, m, sent[half]))

    def all_sp2(ref, m, sent):
        return both(lambda half: sp2(ref, half, m, sent[half]))

    def settle(sent):
        for copies in sent:
            wait_all(copies)

    quarter = sub // 4
    cuts = [pl.ds(i * quarter, quarter) for i in range(4)]
    order = (0, 2, 1, 3)
    k_own = (3 * pipe, 1 + pipe)
    k_got = (3 * other, 1 + other)
    for copy in own_load:
        copy.wait()
    e0 = {i: remote(own.at[pipe, cuts[i], :], w.at[3 * pipe, core, z, cuts[i], :], pair) for i in order}
    e1 = remote(own.at[other], w.at[1 + pipe, core, z], pair)
    ca0 = g1(k_own[0])
    for copy in x_load:
        copy.wait()
    x_here, x_swap = swap_tokens(0, x0)
    ca1 = {}
    for i in order:
        e0[i].wait_recv()
        ca1[i] = g1(k_got[0], cuts[i])
    wait_all(ca0)
    cb0 = g2(k_own[0])
    cc0 = g2c(k_own[0])
    cb1 = []
    for i in order:
        wait_all(ca1[i])
        ahead, to, dev = (zd, up, "u") if i < 2 else (zu, dn, "d")
        cb1.append(same(w.at[k_got[0], core, ahead, cuts[i], :], to))
    cc1 = g2c(k_got[0])
    for copy in cot_load:
        copy.wait()
    cot_here, cot_swap = swap_tokens(1, cot)
    ca2 = g1(k_own[1])
    e1.wait_recv()
    ca3 = g1(k_got[1])
    wait_all(cb0)
    cd0 = g3(k_own[0])
    wait_all(cb1)
    cd1 = g3(k_got[0])
    x_here.wait()
    wait_all(x_swap)
    wait_all(cc0 + cc1)
    wait_all(cd0 + cd1)

    p00 = project_send(x0, 0, 0, 0)
    p01 = project_send(x0, 0, 0, 1)
    cot_here.wait()
    wait_all(cot_swap)
    project(cot, 3, 2, 0, 0)
    project(cot, 3, 2, 1, 0)
    p00 = all_rs2(0, 0, p00)
    wait_all(ca2)
    cb2 = g2(k_own[1])
    cc2 = g2c(k_own[1])
    project(cot, 3, 2, 0, 1)
    p01 = all_rs2(0, 1, p01)

    def open_act(m, sent):
        done = []
        for half in HALVES:
            pre = units(0, half, m, sent[half])
            keep[0, half, slots(m), :] = pre
            put(act.at[0], half, m, jax.nn.silu(pre).astype(BF))
            done.append(sp1(act.at[0], half, m))
        return done

    a00 = open_act(0, p00)
    project(cot, 3, 2, 1, 1)
    a01 = open_act(1, p01)
    a00 = all_sp2(act.at[0], 0, a00)
    a01 = all_sp2(act.at[0], 1, a01)
    p20 = both(lambda half: rs1(2, half, 0))
    p21 = both(lambda half: rs1(2, half, 1))
    wait_all(ca3)
    cb3 = g2(k_got[1])
    cc3 = g2c(k_got[1])
    wait_all(cb2)
    cd2 = g3(k_own[1])
    settle(a00)
    wait_all(cb3)
    cd3 = g3(k_got[1])
    wait_all(cc2 + cc3)
    wait_all(cd2 + cd3)
    widen(x0, act.at[0], 1, x1, 0)
    p10 = project_send(x1, 2, 1, 0)
    settle(a01)
    widen(x0, act.at[0], 1, x1, 1)
    p11 = project_send(x1, 2, 1, 1)
    p20 = all_rs2(2, 0, p20)
    p21 = all_rs2(2, 1, p21)
    p10 = all_rs2(1, 0, p10)
    p11 = all_rs2(1, 1, p11)

    def open_slope(m, sent_up, sent_pre):
        done = []
        for half in HALVES:
            upward = units(2, half, m, sent_up[half])
            pre = units(1, half, m, sent_pre[half])
            put(slope.at[1], half, m, slope_of(upward, pre))
            done.append(sp1(slope.at[1], half, m))
            put(act.at[1], half, m, jax.nn.silu(pre).astype(BF))
        return done

    s10 = open_slope(0, p20, p10)
    s11 = open_slope(1, p21, p11)
    s10 = all_sp2(slope.at[1], 0, s10)
    s11 = all_sp2(slope.at[1], 1, s11)
    a10 = both(lambda half: sp1(act.at[1], half, 0))
    a11 = both(lambda half: sp1(act.at[1], half, 1))
    settle(s10)
    widen(cot, slope.at[1], 2, err1, 0)
    p30 = project_send(err1, 1, 3, 0)
    settle(s11)
    widen(cot, slope.at[1], 2, err1, 1)
    p31 = project_send(err1, 1, 3, 1)
    a10 = all_sp2(act.at[1], 0, a10)
    d2, near2 = weight_grad(x1, slope.at[1], 2)
    p30 = all_rs2(3, 0, p30)
    p31 = all_rs2(3, 1, p31)
    a11 = all_sp2(act.at[1], 1, a11)
    d1, near1 = weight_grad(err1, act.at[0], 1)

    def close_slope(m, sent):
        done = []
        for half in HALVES:
            upward = units(3, half, m, sent[half])
            put(slope.at[0], half, m, slope_of(upward, keep[0, half, slots(m), :]))
            done.append(sp1(slope.at[0], half, m))
        return done

    s00 = close_slope(0, p30)
    s01 = close_slope(1, p31)
    d2 = q2(2, d2, near2)
    s00 = all_sp2(slope.at[0], 0, s00)
    s01 = all_sp2(slope.at[0], 1, s01)
    settle(a10)
    settle(a11)
    d3, near3 = weight_grad(cot, act.at[1], 3)
    d1 = q2(1, d1, near1)
    settle(s00)
    settle(s01)
    d0, near0 = weight_grad(x0, slope.at[0], 0)
    d3 = q2(3, d3, near3)
    squares = finish(2, d2)
    squares = squares + finish(1, d1)
    d0 = q2(0, d0, near0)
    squares = squares + finish(3, d3)
    h1 = hand_over(1)
    turned[0] = fin[2 * pipe + 1].T
    writes = [local(turned.at[0], tot_out.at[:, keep_rows])]
    squares = squares + finish(0, d0)
    nsum[0] = squares
    c1 = [remote(nsum.at[0], n2.at[code], dev) for code, dev in xz]
    h0 = hand_over(0)
    writes.append(local(fin.at[2 * pipe], tot_in.at[keep_rows, :]))
    wait_all(c1)
    total = nsum[0]
    for code in range(1, 16):
        total = total + n2[code]
    nsum[1] = total
    c2 = [remote(nsum.at[1], n1.at[code], dev) for code, dev, _, _ in ycore]
    h1.wait_recv()
    turned[1] = prx[1].astype(F32).T
    writes.append(local(turned.at[1], tot_out.at[:, give_rows]))
    wait_all(c2)
    total = nsum[1]
    for code in range(1, 8):
        total = total + n1[code]
    norm = jnp.sqrt(jnp.sum(total, keepdims=True))
    norm_out[...] = jnp.broadcast_to(norm, norm_out.shape)
    h0.wait_recv()
    late[...] = prx[0].astype(F32)
    writes.append(local(late, tot_in.at[give_rows, :]))
    for copy in started:
        copy.wait_send()
    for copy in writes:
        copy.wait()


def on_device(inputs, w_in, w_out, cotangent):
    micro, tok, cols = inputs.shape
    shard, hid = w_in.shape[1], w_in.shape[2]
    sub = shard // 2
    part_d = cols // 4
    group = micro * tok // 2
    hl = hid // 2
    any_spec = pl.BlockSpec(memory_space=pl.ANY)
    vmem = pl.BlockSpec(memory_space=pltpu.VMEM)
    tokens = pltpu.VMEM((RING, micro, tok // 2, part_d), BF)
    weights = pltpu.VMEM((4, 2, RING, sub, hid), BF)
    layers = pltpu.VMEM((2, RING, group, hid), BF)
    tot_in, tot_out, norm = pl.pallas_call(
        kernel,
        out_shape=(
            jax.ShapeDtypeStruct((shard, hid), F32),
            jax.ShapeDtypeStruct((hid, shard), F32),
            jax.ShapeDtypeStruct((8, 128), F32),
        ),
        in_specs=[any_spec] * 4,
        out_specs=(any_spec, any_spec, vmem),
        scratch_shapes=[
            pltpu.VMEM((2, RING, micro, tok, RING * sub), BF),
            tokens, tokens, tokens, tokens,
            pltpu.VMEM((2, hid, sub), BF),
            pltpu.VMEM((2, sub, hid), BF),
            weights, weights, layers, layers,
            pltpu.VMEM((4, RING, group, hid), BF),
            pltpu.VMEM((4, 2, RING, group, hl), BF),
            pltpu.VMEM((4, 2, RING, group // RING, hl), BF),
            pltpu.VMEM((2, 2, group // RING, hl), F32),
            pltpu.VMEM((4, RING, sub, hid), BF),
            pltpu.VMEM((4, 2, sub // 2, hid), BF),
            pltpu.VMEM((4, 2, sub, hid), BF),
            pltpu.VMEM((4, sub, hid), F32),
            pltpu.VMEM((2, sub, hid), BF),
            pltpu.VMEM((2, sub, hid), BF),
            pltpu.VMEM((sub, hid), F32),
            pltpu.VMEM((2, hid, sub), F32),
            pltpu.VMEM((2, 8, 128), F32),
            pltpu.VMEM((8, 8, 128), F32),
            pltpu.VMEM((16, 8, 128), F32),
            pltpu.SemaphoreType.DMA((48,)),
            pltpu.SemaphoreType.DMA((320,)),
            pltpu.SemaphoreType.DMA((320,)),
        ],
        compiler_params=pltpu.CompilerParams(
            collective_id=0, has_side_effects=True, vmem_limit_bytes=67043328
        ),
    )(inputs, w_in[0], w_out[0], cotangent)
    grad_norm = norm[0, 0]
    factor = jnp.minimum(1.0, CLIP_NORM / grad_norm)
    return (tot_in * factor)[None], (tot_out * factor)[None], grad_norm


def solution(mesh):
    split = Mesh(mesh.devices.reshape(mesh.shape["pipe"], 2, 2, RING, RING), AXES)
    placed = (
        P(None, DP, TENSOR),
        P("pipe", TENSOR_DP, None),
        P("pipe", None, TENSOR_DP),
        P(None, DP, TENSOR),
    )
    return jax.shard_map(
        on_device,
        mesh=split,
        in_specs=placed,
        out_specs=(P("pipe", TENSOR_DP, None), P("pipe", None, TENSOR_DP), P()),
        check_vma=False,
    )
```

time: 156 us -> 146 us (0.936)
  Pallas kernels: 148 us -> 140 us
  local copies, waits for them, and re-layouts: 6.83 us -> 1.29 us
  other arithmetic: 0 us -> 3.34 us
    pallas_call x1, Pallas kernels: 148 us -> 140 us  [on_device(): pl.pallas_call(kernel, out_shape=(jax.ShapeDtypeStruct((shard, hid), F32)...]
    unnamed x5 -> x2, local copies, waits for them, and re-layouts: 5.55 us -> 0.01 us
    broadcast_in_dim x0 -> x2, other arithmetic: none -> 3.34 us  [on_device(): return ((tot_in * factor)[None], (tot_out * factor)[None], grad_norm)]
where the time goes in v4:
time: 146 us
  Pallas kernels  140 us (96%)
  other arithmetic  3.34 us (2%)
    pallas_call x1, Pallas kernels, on_device(): pl.pallas_call(kernel, out_shape=(jax.ShapeDtypeStruct((shard, hid), F32)...  140 us
    broadcast_in_dim x2, other arithmetic, on_device(): return ((tot_in * factor)[None], (tot_out * factor)[None], grad_norm)  3.34 us

profile of v4, /device:TPU:1, one launch (start us, length us, event | category | flops | bytes accessed | tf_op | source)
XLA Modules:
  0.0 145.9 jit_solution(11867655306622507325)
XLA Ops:
  0.6 139.9 %shard_map.67 = (f32[256,1024]{1,0:T(8,128)}, f32[1024,256]{1,0:T(8,128)}, f32[8,128]{1,0:T(8,128)}) custom-call(bf16[2,128,4096]{2,1,0:T(8,128)(2,1)} %x_hbm.1, bf16[256,1024]{1,0:T(8,128)(2,1)} %bitcast.7, bf16[1024,256]{1,0:T(8,128)(2,1)} %bitcast.8, bf16[2,128,4096]{2,1,0:T(8,128)(2,1)} %cot_hbm.1), custom_call_target="tpu_custom_call" | custom-call | tf_op jit(solution)/shard_map/pallas_call | solution.py:522
  140.6 0.0 copy-start
  140.6 1.3 slice.3
  142.6 2.3 %multiply_bitcast_fusion.1 = f32[1,256,1024]{2,1,0:T(8,128)} fusion(f32[256,1024]{1,0:T(8,128)} %get-tuple-element.6, f32[]{:T(128)S(6)} %min_shard_map.3), kind=kLoop, calls=%fused_computation.1 | loop fusion | flops 262144 | bytes 2097156 | tf_op jit(solution)/shard_map/broadcast_in_dim | solution.py:562
  144.9 0.0 copy-done
  144.9 1.0 multiply_bitcast_fusion
Async XLA Ops:
  140.6 4.3 %copy-start = (f32[1024,256]{1,0:T(8,128)S(1)}, f32[1024,256]{1,0:T(8,128)}, u32[]{:S(2)}) copy-start(f32[1024,256]{1,0:T(8,128)} %get-tuple-element.8) | copy-start | bytes 3145732

commit v5 on v4

--- a/solution.py
+++ b/solution.py
@@ -53,26 +53,57 @@
     count = [0]
     lcount = [0]
 
+    class Group:
+        def __init__(self, like):
+            i = count[0]
+            count[0] += 1
+            self.sems = {"send_sem": ssem.at[i], "recv_sem": rsem.at[i]}
+            self.like = like
+
+        def send(self, src, dst, dev):
+            pltpu.make_async_remote_copy(
+                src_ref=src, dst_ref=dst, device_id=dev, device_id_type=MESH, **self.sems
+            ).start()
+            if self not in started:
+                self.whole = pltpu.make_async_remote_copy(
+                    src_ref=self.like, dst_ref=self.like, device_id=dev, device_id_type=MESH, **self.sems
+                )
+                started.append(self)
+            return self
+
+        def wait_recv(self):
+            self.whole.wait_recv()
+
+        def wait_send(self):
+            self.whole.wait_send()
+
     def remote(src, dst, dev):
-        i = count[0]
-        count[0] += 1
-        copy = pltpu.make_async_remote_copy(
-            src_ref=src, dst_ref=dst, send_sem=ssem.at[i], recv_sem=rsem.at[i],
-            device_id=dev, device_id_type=MESH,
-        )
-        copy.start()
-        started.append(copy)
-        return copy
+        return Group(src).send(src, dst, dev)
 
     def same(ref, dev):
         return remote(ref, ref, dev)
 
+    def group_of(like, items):
+        made = Group(like)
+        for src, dst, dev in items:
+            made.send(src, dst, dev)
+        return [made]
+
+    class Local:
+        def __init__(self, like):
+            self.sem = lsem.at[lcount[0]]
+            lcount[0] += 1
+            self.whole = pltpu.make_async_copy(like, like, self.sem)
+
+        def start(self, src, dst):
+            pltpu.make_async_copy(src, dst, self.sem).start()
+            return self
+
+        def wait(self):
+            self.whole.wait()
+
     def local(src, dst):
-        i = lcount[0]
-        lcount[0] += 1
-        copy = pltpu.make_async_copy(src, dst, lsem.at[i])
-        copy.start()
-        return copy
+        return Local(dst).start(src, dst)
 
     def wait_all(copies):
         for copy in copies:
@@ -108,13 +139,11 @@
     ]
 
     def fetch(src, n):
-        copies = []
+        copies = Local(stage.at[n])
         for yy in range(RING):
             for zz in range(RING):
                 off = pl.multiple_of((zz * RING + yy) * 2 * sub + pipe * sub, sub)
-                copies.append(
-                    local(src.at[:, :, pl.ds(off, sub)], stage.at[n, yy, :, :, pl.ds(zz * sub, sub)])
-                )
+                copies.start(src.at[:, :, pl.ds(off, sub)], stage.at[n, yy, :, :, pl.ds(zz * sub, sub)])
         return copies
 
     x_load = fetch(x_hbm, 0)
@@ -139,23 +168,23 @@
             return stage.at[n, yy, :, toks, :]
 
         landing = dst.at[y, :, :, my_cols]
-        return local(piece(y, core), landing), [
-            remote(piece(yy, cc), landing, dev) for _, dev, yy, cc in ycore
-        ]
+        return local(piece(y, core), landing), group_of(
+            r1.at[n, pl.ds(1, 7)], [(piece(yy, cc), landing, dev) for _, dev, yy, cc in ycore]
+        )
 
     lo, hi = pl.ds(0, hs), pl.ds(hs, hs)
 
     def g1(k, rows_of=slice(None)):
         ref = w.at[k, core, z, rows_of, :]
-        return [same(ref, up), same(ref, dn)]
-
-    def g2(k, cuts=(lo, hi)):
-        ring = [same(w.at[k, core, zd, r, :], up) for r in cuts[: len(cuts) // 2]]
-        ring += [same(w.at[k, core, zu, r, :], dn) for r in cuts[len(cuts) // 2 :]]
-        return ring
+        return group_of(w.at[k, core, pl.ds(0, 2), rows_of, :], [(ref, ref, up), (ref, ref, dn)])
+
+    def g2(k):
+        a, b = w.at[k, core, zd, lo, :], w.at[k, core, zu, hi, :]
+        return group_of(w.at[k, core, z], [(a, a, up), (b, b, dn)])
 
     def g2c(k):
-        return [same(w.at[k, core, at], twin) for at in (z, zu, zd)]
+        refs = [w.at[k, core, at] for at in (z, zu, zd)]
+        return group_of(w.at[k, core, pl.ds(0, 3)], [(ref, ref, twin) for ref in refs])
 
     def g3(k):
         return [same(w.at[k, core, z2], twin)]
@@ -228,24 +257,33 @@
     def slots(m):
         return pl.ds(m * crows, crows)
 
+    def r1_at(half, slot):
+        return half * RING + slot
+
     def rs1(ph, half, m):
         lanes, r = halves[half], streams[m]
-        return [
-            remote(part.at[ph, at, r, lanes], r1.at[ph, half, slot, r], dev)
-            for slot, dev, at in first[half]
-        ]
+        return group_of(
+            r1.at[ph, pl.ds(r1_at(half, 1), 3), r],
+            [
+                (part.at[ph, at, r, lanes], r1.at[ph, r1_at(half, slot), r], dev)
+                for slot, dev, at in first[half]
+            ],
+        )
 
     def rs2(ph, half, m, copies):
         wait_all(copies)
         lanes, r = halves[half], streams[m]
         b = block[half]
         part[ph, b, r, lanes] = plus(
-            part[ph, b, r, lanes], r1[ph, half, 1, r], r1[ph, half, 2, r], r1[ph, half, 3, r]
+            part[ph, b, r, lanes], *[r1[ph, r1_at(half, slot), r] for slot in (1, 2, 3)]
         ).astype(BF)
-        return [
-            remote(part.at[ph, b, inner_rows(at, m), lanes], r2.at[ph, half, slot, slots(m)], dev)
-            for slot, dev, at in second[half]
-        ]
+        return group_of(
+            r2.at[ph, half, pl.ds(1, 3), slots(m)],
+            [
+                (part.at[ph, b, inner_rows(at, m), lanes], r2.at[ph, half, slot, slots(m)], dev)
+                for slot, dev, at in second[half]
+            ],
+        )
 
     def units(ph, half, m, copies):
         wait_all(copies)
@@ -260,12 +298,14 @@
 
     def sp1(ref, half, m):
         piece = ref.at[block[half], inner_rows(inner[half], m), halves[half]]
-        return [same(piece, dev) for _, dev, _ in second[half]]
+        like = ref.at[block[half], pl.ds(m * mrows, 3 * crows), halves[half]]
+        return group_of(like, [(piece, piece, dev) for _, dev, _ in second[half]])
 
     def sp2(ref, half, m, copies):
         wait_all(copies)
         piece = ref.at[block[half], streams[m], halves[half]]
-        return [same(piece, dev) for _, dev, _ in first[half]]
+        like = ref.at[pl.ds(0, 3), streams[m], halves[half]]
+        return group_of(like, [(piece, piece, dev) for _, dev, _ in first[half]])
 
     def slope_of(upward, pre):
         sig = jax.nn.sigmoid(pre)
@@ -274,10 +314,13 @@
     def q1(k, copies):
         wait_all(copies)
         g[k, core, z2] = plus(g[k, core, z2], rc[k, z2]).astype(BF)
-        return [
-            remote(g.at[k, core, z2, lo, :], ra.at[k, 0], up),
-            remote(g.at[k, core, z2, hi, :], ra.at[k, 1], dn),
-        ]
+        return group_of(
+            ra.at[k],
+            [
+                (g.at[k, core, z2, lo, :], ra.at[k, 0], up),
+                (g.at[k, core, z2, hi, :], ra.at[k, 1], dn),
+            ],
+        )
 
     def q2(k, copies, near):
         near.wait_recv()
@@ -286,10 +329,9 @@
         wait_all(copies)
         g[k, core, zu, lo, :] = plus(g[k, core, zu, lo, :], rc[k, zu, lo, :], ra[k, 0]).astype(BF)
         g[k, core, zd, hi, :] = plus(g[k, core, zd, hi, :], rc[k, zd, hi, :], ra[k, 1]).astype(BF)
-        return [
-            remote(g.at[k, core, zu], rb.at[k, 0], up),
-            remote(g.at[k, core, zd], rb.at[k, 1], dn),
-        ]
+        return group_of(
+            rb.at[k], [(g.at[k, core, zu], rb.at[k, 0], up), (g.at[k, core, zd], rb.at[k, 1], dn)]
+        )
 
     def fold(value):
         lanes = value.shape[-1]
@@ -341,9 +383,10 @@
     e0 = {i: remote(own.at[pipe, cuts[i], :], w.at[3 * pipe, core, z, cuts[i], :], pair) for i in order}
     e1 = remote(own.at[other], w.at[1 + pipe, core, z], pair)
     ca0 = g1(k_own[0])
-    for copy in x_load:
-        copy.wait()
+    x_load.wait()
     x_here, x_swap = swap_tokens(0, x0)
+    cot_load.wait()
+    cot_here, cot_swap = swap_tokens(1, cot)
     ca1 = {}
     for i in order:
         e0[i].wait_recv()
@@ -351,21 +394,19 @@
     wait_all(ca0)
     cb0 = g2(k_own[0])
     cc0 = g2c(k_own[0])
-    cb1 = []
+    cb1 = Group(w.at[k_got[0], core, z])
     for i in order:
         wait_all(ca1[i])
-        ahead, to, dev = (zd, up, "u") if i < 2 else (zu, dn, "d")
-        cb1.append(same(w.at[k_got[0], core, ahead, cuts[i], :], to))
+        ahead, to = (zd, up) if i < 2 else (zu, dn)
+        ref = w.at[k_got[0], core, ahead, cuts[i], :]
+        cb1.send(ref, ref, to)
     cc1 = g2c(k_got[0])
-    for copy in cot_load:
-        copy.wait()
-    cot_here, cot_swap = swap_tokens(1, cot)
     ca2 = g1(k_own[1])
     e1.wait_recv()
     ca3 = g1(k_got[1])
     wait_all(cb0)
     cd0 = g3(k_own[0])
-    wait_all(cb1)
+    cb1.wait_recv()
     cd1 = g3(k_got[0])
     x_here.wait()
     wait_all(x_swap)
@@ -374,15 +415,18 @@
 
     p00 = project_send(x0, 0, 0, 0)
     p01 = project_send(x0, 0, 0, 1)
-    cot_here.wait()
-    wait_all(cot_swap)
-    project(cot, 3, 2, 0, 0)
-    project(cot, 3, 2, 1, 0)
-    p00 = all_rs2(0, 0, p00)
     wait_all(ca2)
     cb2 = g2(k_own[1])
     cc2 = g2c(k_own[1])
-    project(cot, 3, 2, 0, 1)
+    cot_here.wait()
+    wait_all(cot_swap)
+    for m in (0, 1):
+        for half in HALVES:
+            project(cot, 3, 2, half, m)
+    p00 = all_rs2(0, 0, p00)
+    wait_all(ca3)
+    cb3 = g2(k_got[1])
+    cc3 = g2c(k_got[1])
     p01 = all_rs2(0, 1, p01)
 
     def open_act(m, sent):
@@ -395,22 +439,18 @@
         return done
 
     a00 = open_act(0, p00)
-    project(cot, 3, 2, 1, 1)
     a01 = open_act(1, p01)
     a00 = all_sp2(act.at[0], 0, a00)
     a01 = all_sp2(act.at[0], 1, a01)
     p20 = both(lambda half: rs1(2, half, 0))
     p21 = both(lambda half: rs1(2, half, 1))
-    wait_all(ca3)
-    cb3 = g2(k_got[1])
-    cc3 = g2c(k_got[1])
     wait_all(cb2)
     cd2 = g3(k_own[1])
-    settle(a00)
     wait_all(cb3)
     cd3 = g3(k_got[1])
     wait_all(cc2 + cc3)
     wait_all(cd2 + cd3)
+    settle(a00)
     widen(x0, act.at[0], 1, x1, 0)
     p10 = project_send(x1, 2, 1, 0)
     settle(a01)
@@ -449,6 +489,7 @@
     p31 = all_rs2(3, 1, p31)
     a11 = all_sp2(act.at[1], 1, a11)
     d1, near1 = weight_grad(err1, act.at[0], 1)
+    d2 = q2(2, d2, near2)
 
     def close_slope(m, sent):
         done = []
@@ -460,7 +501,6 @@
 
     s00 = close_slope(0, p30)
     s01 = close_slope(1, p31)
-    d2 = q2(2, d2, near2)
     s00 = all_sp2(slope.at[0], 0, s00)
     s01 = all_sp2(slope.at[0], 1, s01)
     settle(a10)
@@ -480,7 +520,7 @@
     writes = [local(turned.at[0], tot_out.at[:, keep_rows])]
     squares = squares + finish(0, d0)
     nsum[0] = squares
-    c1 = [remote(nsum.at[0], n2.at[code], dev) for code, dev in xz]
+    c1 = group_of(n2.at[pl.ds(1, 15)], [(nsum.at[0], n2.at[code], dev) for code, dev in xz])
     h0 = hand_over(0)
     writes.append(local(fin.at[2 * pipe], tot_in.at[keep_rows, :]))
     wait_all(c1)
@@ -488,7 +528,7 @@
     for code in range(1, 16):
         total = total + n2[code]
     nsum[1] = total
-    c2 = [remote(nsum.at[1], n1.at[code], dev) for code, dev, _, _ in ycore]
+    c2 = group_of(n1.at[pl.ds(1, 7)], [(nsum.at[1], n1.at[code], dev) for code, dev, _, _ in ycore])
     h1.wait_recv()
     turned[1] = prx[1].astype(F32).T
     writes.append(local(turned.at[1], tot_out.at[:, give_rows]))
@@ -497,7 +537,7 @@
     for code in range(1, 8):
         total = total + n1[code]
     norm = jnp.sqrt(jnp.sum(total, keepdims=True))
-    norm_out[...] = jnp.broadcast_to(norm, norm_out.shape)
+    norm_out[...] = norm
     h0.wait_recv()
     late[...] = prx[0].astype(F32)
     writes.append(local(late, tot_in.at[give_rows, :]))
@@ -524,7 +564,7 @@
         out_shape=(
             jax.ShapeDtypeStruct((shard, hid), F32),
             jax.ShapeDtypeStruct((hid, shard), F32),
-            jax.ShapeDtypeStruct((8, 128), F32),
+            jax.ShapeDtypeStruct((1, 1), F32),
         ),
         in_specs=[any_spec] * 4,
         out_specs=(any_spec, any_spec, vmem),
@@ -535,7 +575,7 @@
             pltpu.VMEM((2, sub, hid), BF),
             weights, weights, layers, layers,
             pltpu.VMEM((4, RING, group, hid), BF),
-            pltpu.VMEM((4, 2, RING, group, hl), BF),
+            pltpu.VMEM((4, 2 * RING, group, hl), BF),
             pltpu.VMEM((4, 2, RING, group // RING, hl), BF),
             pltpu.VMEM((2, 2, group // RING, hl), F32),
             pltpu.VMEM((4, RING, sub, hid), BF),
@@ -549,9 +589,9 @@
             pltpu.VMEM((2, 8, 128), F32),
             pltpu.VMEM((8, 8, 128), F32),
             pltpu.VMEM((16, 8, 128), F32),
-            pltpu.SemaphoreType.DMA((48,)),
-            pltpu.SemaphoreType.DMA((320,)),
-            pltpu.SemaphoreType.DMA((320,)),
+            pltpu.SemaphoreType.DMA((12,)),
+            pltpu.SemaphoreType.DMA((110,)),
+            pltpu.SemaphoreType.DMA((110,)),
         ],
         compiler_params=pltpu.CompilerParams(
             collective_id=0, has_side_effects=True, vmem_limit_bytes=67043328

time: 146 us -> 139 us (0.952)
  Pallas kernels: 140 us -> 132 us
  between operations: 1.34 us -> 3.14 us
    pallas_call x1, Pallas kernels: 140 us -> 132 us  [on_device(): pl.pallas_call(kernel, out_shape=(jax.ShapeDtypeStruct((shard, hid), F32)...]
where the time goes in v5:
time: 139 us
  Pallas kernels  132 us (95%)
  other arithmetic  3.34 us (2%)
  between operations  3.14 us (2%)
    pallas_call x1, Pallas kernels, on_device(): pl.pallas_call(kernel, out_shape=(jax.ShapeDtypeStruct((shard, hid), F32)...  132 us
    broadcast_in_dim x2, other arithmetic, on_device(): return ((tot_in * factor)[None], (tot_out * factor)[None], grad_norm)  3.34 us

profile of v5, /device:TPU:1, one launch (start us, length us, event | category | flops | bytes accessed | tf_op | source)
XLA Modules:
  0.0 138.9 jit_solution(6782239198976124068)
XLA Ops:
  0.6 132.4 %shard_map.67 = (f32[256,1024]{1,0:T(8,128)}, f32[1024,256]{1,0:T(8,128)}, f32[1,1]{1,0:T(1,128)}) custom-call(bf16[2,128,4096]{2,1,0:T(8,128)(2,1)} %x_hbm.1, bf16[256,1024]{1,0:T(8,128)(2,1)} %bitcast.7, bf16[1024,256]{1,0:T(8,128)(2,1)} %bitcast.8, bf16[2,128,4096]{2,1,0:T(8,128)(2,1)} %cot_hbm.1), custom_call_target="tpu_custom_call" | custom-call | tf_op jit(solution)/shard_map/pallas_call | solution.py:562
  133.1 0.0 copy-start
  133.8 2.3 %multiply_bitcast_fusion.1 = f32[1,256,1024]{2,1,0:T(8,128)} fusion(f32[256,1024]{1,0:T(8,128)} %get-tuple-element.6, f32[]{:T(128)S(6)} %min_shard_map.3), kind=kLoop, calls=%fused_computation.1 | loop fusion | flops 262144 | bytes 2097156 | tf_op jit(solution)/shard_map/broadcast_in_dim | solution.py:602
  136.1 0.0 copy-done
  136.1 1.0 multiply_bitcast_fusion
Async XLA Ops:
  133.1 3.1 %copy-start = (f32[1024,256]{1,0:T(8,128)S(1)}, f32[1024,256]{1,0:T(8,128)}, u32[]{:S(2)}) copy-start(f32[1024,256]{1,0:T(8,128)} %get-tuple-element.8) | copy-start | bytes 3145732

commit v6 on v5

--- a/solution.py
+++ b/solution.py
@@ -25,7 +25,7 @@
     x_hbm, win_hbm, wout_hbm, cot_hbm,
     tot_in, tot_out, norm_out,
     stage, x0, cot, x1, err1, raw, own, w, g, act, slope,
-    part, r1, r2, keep,
+    part, r1, rx, r2, keep,
     rc, ra, rb,
     fin, pex, prx, late, turned, nsum, n1, n2,
     lsem, ssem, rsem,
@@ -234,9 +234,8 @@
         side(core2, p_near)
         near = across(p_near)
         side(core, p_far)
-        sent = q1(k, [far])
         side(core, p_near)
-        return sent, near
+        return q1(k, [far]), near
 
     def plus(x, *more):
         total = x.astype(F32)
@@ -285,6 +284,21 @@
             ],
         )
 
+    def rs1_turned(ph, m):
+        return group_of(
+            rx.at[pl.ds(1, 3)],
+            [(part.at[ph, :, inner_rows(at, m), halves[1]], rx.at[slot], dev) for slot, dev, at in xpeers],
+        )
+
+    def rs2_turned(ph, m, copies):
+        wait_all(copies)
+        mid = inner_rows(xi, m)
+        part[ph, :, mid, halves[1]] = plus(part[ph, :, mid, halves[1]], rx[1], rx[2], rx[3]).astype(BF)
+        return group_of(
+            r2.at[ph, 1, pl.ds(1, 3), slots(m)],
+            [(part.at[ph, at, mid, halves[1]], r2.at[ph, 1, slot, slots(m)], dev) for slot, dev, at in ypeers],
+        )
+
     def units(ph, half, m, copies):
         wait_all(copies)
         c = slots(m)
@@ -376,59 +390,6 @@
     quarter = sub // 4
     cuts = [pl.ds(i * quarter, quarter) for i in range(4)]
     order = (0, 2, 1, 3)
-    k_own = (3 * pipe, 1 + pipe)
-    k_got = (3 * other, 1 + other)
-    for copy in own_load:
-        copy.wait()
-    e0 = {i: remote(own.at[pipe, cuts[i], :], w.at[3 * pipe, core, z, cuts[i], :], pair) for i in order}
-    e1 = remote(own.at[other], w.at[1 + pipe, core, z], pair)
-    ca0 = g1(k_own[0])
-    x_load.wait()
-    x_here, x_swap = swap_tokens(0, x0)
-    cot_load.wait()
-    cot_here, cot_swap = swap_tokens(1, cot)
-    ca1 = {}
-    for i in order:
-        e0[i].wait_recv()
-        ca1[i] = g1(k_got[0], cuts[i])
-    wait_all(ca0)
-    cb0 = g2(k_own[0])
-    cc0 = g2c(k_own[0])
-    cb1 = Group(w.at[k_got[0], core, z])
-    for i in order:
-        wait_all(ca1[i])
-        ahead, to = (zd, up) if i < 2 else (zu, dn)
-        ref = w.at[k_got[0], core, ahead, cuts[i], :]
-        cb1.send(ref, ref, to)
-    cc1 = g2c(k_got[0])
-    ca2 = g1(k_own[1])
-    e1.wait_recv()
-    ca3 = g1(k_got[1])
-    wait_all(cb0)
-    cd0 = g3(k_own[0])
-    cb1.wait_recv()
-    cd1 = g3(k_got[0])
-    x_here.wait()
-    wait_all(x_swap)
-    wait_all(cc0 + cc1)
-    wait_all(cd0 + cd1)
-
-    p00 = project_send(x0, 0, 0, 0)
-    p01 = project_send(x0, 0, 0, 1)
-    wait_all(ca2)
-    cb2 = g2(k_own[1])
-    cc2 = g2c(k_own[1])
-    cot_here.wait()
-    wait_all(cot_swap)
-    for m in (0, 1):
-        for half in HALVES:
-            project(cot, 3, 2, half, m)
-    p00 = all_rs2(0, 0, p00)
-    wait_all(ca3)
-    cb3 = g2(k_got[1])
-    cc3 = g2c(k_got[1])
-    p01 = all_rs2(0, 1, p01)
-
     def open_act(m, sent):
         done = []
         for half in HALVES:
@@ -438,29 +399,83 @@
             done.append(sp1(act.at[0], half, m))
         return done
 
+    own1, got1 = 1 + pipe, 1 + other
+    for copy in own_load:
+        copy.wait()
+    e0 = {i: remote(own.at[pipe, cuts[i], :], w.at[3 * pipe, core, z, cuts[i], :], pair) for i in order}
+    e1 = remote(own.at[other], w.at[own1, core, z], pair)
+    x_load.wait()
+    x_here, x_swap = swap_tokens(0, x0)
+    ca_own1 = g1(own1, lo)
+    cot_load.wait()
+    cot_here, cot_swap = swap_tokens(1, cot)
+    ca0 = {}
+    for i in order:
+        e0[i].wait_recv()
+        ca0[i] = g1(0, cuts[i])
+    cb0 = Group(w.at[0, core, z])
+    for i in order:
+        wait_all(ca0[i])
+        ahead, to = (zd, up) if i < 2 else (zu, dn)
+        ref = w.at[0, core, ahead, cuts[i], :]
+        cb0.send(ref, ref, to)
+    cc0 = g2c(0)
+    ca3 = g1(3)
+    ca_own1 += g1(own1, hi)
+    e1.wait_recv()
+    ca_got1 = g1(got1)
+    cb0.wait_recv()
+    cd0 = g3(0)
+    x_here.wait()
+    wait_all(x_swap)
+    wait_all(cc0)
+    wait_all(cd0)
+
+    project(x0, 0, 0, 0, 0)
+    p00a = rs1(0, 0, 0)
+    project(x0, 0, 0, 1, 0)
+    p00b = rs1_turned(0, 0)
+    p01 = project_send(x0, 0, 0, 1)
+    wait_all(ca3)
+    cb3 = g2(3)
+    cc3 = g2c(3)
+    wait_all(ca_own1)
+    cb_own1 = g2(own1)
+    cc_own1 = g2c(own1)
+    p00 = [rs2(0, 0, 0, p00a), rs2_turned(0, 0, p00b)]
+    p01 = all_rs2(0, 1, p01)
     a00 = open_act(0, p00)
+    wait_all(ca_got1)
+    cb_got1 = g2(got1)
+    cc_got1 = g2c(got1)
     a01 = open_act(1, p01)
     a00 = all_sp2(act.at[0], 0, a00)
+    wait_all(cb3)
+    cd3 = g3(3)
     a01 = all_sp2(act.at[0], 1, a01)
-    p20 = both(lambda half: rs1(2, half, 0))
-    p21 = both(lambda half: rs1(2, half, 1))
-    wait_all(cb2)
-    cd2 = g3(k_own[1])
-    wait_all(cb3)
-    cd3 = g3(k_got[1])
-    wait_all(cc2 + cc3)
-    wait_all(cd2 + cd3)
+    cot_here.wait()
+    wait_all(cot_swap)
+    wait_all(cc3)
+    wait_all(cd3)
+    p20 = project_send(cot, 3, 2, 0)
+    wait_all(cb_own1)
+    cd_own1 = g3(own1)
+    project(cot, 3, 2, 0, 1)
+    project(cot, 3, 2, 1, 1)
+    wait_all(cb_got1)
+    cd_got1 = g3(got1)
     settle(a00)
+    wait_all(cc_own1 + cc_got1)
+    wait_all(cd_own1 + cd_got1)
     widen(x0, act.at[0], 1, x1, 0)
     p10 = project_send(x1, 2, 1, 0)
+    p21 = both(lambda half: rs1(2, half, 1))
     settle(a01)
     widen(x0, act.at[0], 1, x1, 1)
     p11 = project_send(x1, 2, 1, 1)
     p20 = all_rs2(2, 0, p20)
+    p10 = all_rs2(1, 0, p10)
     p21 = all_rs2(2, 1, p21)
-    p10 = all_rs2(1, 0, p10)
-    p11 = all_rs2(1, 1, p11)
-
     def open_slope(m, sent_up, sent_pre):
         done = []
         for half in HALVES:
@@ -471,6 +486,7 @@
             put(act.at[1], half, m, jax.nn.silu(pre).astype(BF))
         return done
 
+    p11 = all_rs2(1, 1, p11)
     s10 = open_slope(0, p20, p10)
     s11 = open_slope(1, p21, p11)
     s10 = all_sp2(slope.at[1], 0, s10)
@@ -481,16 +497,13 @@
     widen(cot, slope.at[1], 2, err1, 0)
     p30 = project_send(err1, 1, 3, 0)
     settle(s11)
+    d2, near2 = weight_grad(x1, slope.at[1], 2)
+    a10 = all_sp2(act.at[1], 0, a10)
     widen(cot, slope.at[1], 2, err1, 1)
     p31 = project_send(err1, 1, 3, 1)
-    a10 = all_sp2(act.at[1], 0, a10)
-    d2, near2 = weight_grad(x1, slope.at[1], 2)
     p30 = all_rs2(3, 0, p30)
-    p31 = all_rs2(3, 1, p31)
-    a11 = all_sp2(act.at[1], 1, a11)
     d1, near1 = weight_grad(err1, act.at[0], 1)
     d2 = q2(2, d2, near2)
-
     def close_slope(m, sent):
         done = []
         for half in HALVES:
@@ -500,18 +513,20 @@
         return done
 
     s00 = close_slope(0, p30)
+    p31 = all_rs2(3, 1, p31)
+    a11 = all_sp2(act.at[1], 1, a11)
+    s00 = all_sp2(slope.at[0], 0, s00)
     s01 = close_slope(1, p31)
-    s00 = all_sp2(slope.at[0], 0, s00)
+    d1 = q2(1, d1, near1)
     s01 = all_sp2(slope.at[0], 1, s01)
     settle(a10)
     settle(a11)
     d3, near3 = weight_grad(cot, act.at[1], 3)
-    d1 = q2(1, d1, near1)
+    squares = finish(2, d2)
     settle(s00)
     settle(s01)
     d0, near0 = weight_grad(x0, slope.at[0], 0)
     d3 = q2(3, d3, near3)
-    squares = finish(2, d2)
     squares = squares + finish(1, d1)
     d0 = q2(0, d0, near0)
     squares = squares + finish(3, d3)
@@ -547,6 +562,12 @@
         copy.wait()
 
 
+def clip(norm_ref, tot_in, tot_out, upd_in, upd_out):
+    factor = jnp.minimum(1.0, CLIP_NORM / norm_ref[...])
+    upd_in[...] = tot_in[...] * factor
+    upd_out[...] = tot_out[...] * factor
+
+
 def on_device(inputs, w_in, w_out, cotangent):
     micro, tok, cols = inputs.shape
     shard, hid = w_in.shape[1], w_in.shape[2]
@@ -576,6 +597,7 @@
             weights, weights, layers, layers,
             pltpu.VMEM((4, RING, group, hid), BF),
             pltpu.VMEM((4, 2 * RING, group, hl), BF),
+            pltpu.VMEM((RING, RING, group // 2 // RING, hl), BF),
             pltpu.VMEM((4, 2, RING, group // RING, hl), BF),
             pltpu.VMEM((2, 2, group // RING, hl), F32),
             pltpu.VMEM((4, RING, sub, hid), BF),
@@ -590,16 +612,24 @@
             pltpu.VMEM((8, 8, 128), F32),
             pltpu.VMEM((16, 8, 128), F32),
             pltpu.SemaphoreType.DMA((12,)),
-            pltpu.SemaphoreType.DMA((110,)),
-            pltpu.SemaphoreType.DMA((110,)),
+            pltpu.SemaphoreType.DMA((111,)),
+            pltpu.SemaphoreType.DMA((111,)),
         ],
         compiler_params=pltpu.CompilerParams(
             collective_id=0, has_side_effects=True, vmem_limit_bytes=67043328
         ),
     )(inputs, w_in[0], w_out[0], cotangent)
-    grad_norm = norm[0, 0]
-    factor = jnp.minimum(1.0, CLIP_NORM / grad_norm)
-    return (tot_in * factor)[None], (tot_out * factor)[None], grad_norm
+    steps = 4
+    in_block = pl.BlockSpec((shard // steps, hid), lambda i: (i, 0))
+    out_block = pl.BlockSpec((hid // steps, shard), lambda i: (i, 0))
+    upd_in, upd_out = pl.pallas_call(
+        clip,
+        grid=(steps,),
+        out_shape=(jax.ShapeDtypeStruct((shard, hid), F32), jax.ShapeDtypeStruct((hid, shard), F32)),
+        in_specs=[pl.BlockSpec((1, 1), lambda i: (0, 0)), in_block, out_block],
+        out_specs=(in_block, out_block),
+    )(norm, tot_in, tot_out)
+    return upd_in[None], upd_out[None], norm[0, 0]
 
 
 def solution(mesh):

time: 139 us -> 140 us (level)
  Pallas kernels: 132 us -> 137 us
  other arithmetic: 3.34 us -> 0 us
    pallas_call x0 -> x1, Pallas kernels: none -> 4.49 us  [on_device(): pl.pallas_call(clip, grid=(steps,), out_shape=(jax.ShapeDtypeStruct((shar...]
    broadcast_in_dim x2 -> x0, other arithmetic: 3.34 us -> none  [on_device(): return ((tot_in * factor)[None], (tot_out * factor)[None], grad_norm)]
where the time goes in v6:
time: 140 us
  Pallas kernels  137 us (98%)
  between operations  2.39 us (2%)
    pallas_call x1, Pallas kernels, on_device(): pl.pallas_call(kernel, out_shape=(jax.ShapeDtypeStruct((shard, hid), F32)...  133 us
    pallas_call x1, Pallas kernels, on_device(): pl.pallas_call(clip, grid=(steps,), out_shape=(jax.ShapeDtypeStruct((shar...  4.49 us

profile of v6, /device:TPU:1, one launch (start us, length us, event | category | flops | bytes accessed | tf_op | source)
XLA Modules:
  0.0 139.5 jit_solution(4354449200496161763)
XLA Ops:
  0.6 132.6 %shard_map.67 = (f32[256,1024]{1,0:T(8,128)}, f32[1024,256]{1,0:T(8,128)}, f32[1,1]{1,0:T(1,128)}) custom-call(bf16[2,128,4096]{2,1,0:T(8,128)(2,1)} %x_hbm.1, bf16[256,1024]{1,0:T(8,128)(2,1)} %bitcast.5, bf16[1024,256]{1,0:T(8,128)(2,1)} %bitcast.6, bf16[2,128,4096]{2,1,0:T(8,128)(2,1)} %cot_hbm.1), custom_call_target="tpu_custom_call" | custom-call | tf_op jit(solution)/shard_map/pallas_call | solution.py:583
  133.3 4.5 %shard_map.68 = (f32[256,1024]{1,0:T(8,128)}, f32[1024,256]{1,0:T(8,128)}) custom-call(f32[1,1]{1,0:T(1,128)} %get-tuple-element.8.norm_ref, f32[256,1024]{1,0:T(8,128)} %get-tuple-element.9.tot_in, f32[1024,256]{1,0:T(8,128)} %get-tuple-element.10.tot_out), custom_call_target="tpu_custom_call" | custom-call | tf_op jit(solution)/shard_map/pallas_call | solution.py:625

commit v7 on v6

--- a/solution.py
+++ b/solution.py
@@ -53,38 +53,49 @@
     count = [0]
     lcount = [0]
 
+    class Outbox:
+
+        def __init__(self, like):
+            self.sem = ssem.at[len(started)]
+            self.like = like
+            started.append(self)
+
+        def wait_send(self):
+            sems, dev = self.last
+            pltpu.make_async_remote_copy(
+                src_ref=self.like, dst_ref=self.like, device_id=dev, device_id_type=MESH, **sems
+            ).wait_send()
+
     class Group:
-        def __init__(self, like):
+        def __init__(self, like, outbox=None):
             i = count[0]
             count[0] += 1
-            self.sems = {"send_sem": ssem.at[i], "recv_sem": rsem.at[i]}
-            self.like = like
+            if outbox is None:
+                outbox = Outbox(like)
+            self.sems = {"send_sem": outbox.sem, "recv_sem": rsem.at[i]}
+            self.like, self.outbox = like, outbox
 
         def send(self, src, dst, dev):
             pltpu.make_async_remote_copy(
                 src_ref=src, dst_ref=dst, device_id=dev, device_id_type=MESH, **self.sems
             ).start()
-            if self not in started:
-                self.whole = pltpu.make_async_remote_copy(
-                    src_ref=self.like, dst_ref=self.like, device_id=dev, device_id_type=MESH, **self.sems
-                )
-                started.append(self)
+            self.whole = pltpu.make_async_remote_copy(
+                src_ref=self.like, dst_ref=self.like, device_id=dev, device_id_type=MESH, **self.sems
+            )
+            self.outbox.last = self.sems, dev
             return self
 
         def wait_recv(self):
             self.whole.wait_recv()
 
-        def wait_send(self):
-            self.whole.wait_send()
-
     def remote(src, dst, dev):
         return Group(src).send(src, dst, dev)
 
     def same(ref, dev):
         return remote(ref, ref, dev)
 
-    def group_of(like, items):
-        made = Group(like)
+    def group_of(like, items, outbox=None):
+        made = Group(like, outbox)
         for src, dst, dev in items:
             made.send(src, dst, dev)
         return [made]
@@ -196,32 +207,27 @@
     srows = RING * mrows
 
     def project(src, k, ph, half, m):
-        @pl.loop(0, hl // tile)
-        def _(n):
-            cols = pl.ds(pl.multiple_of(half * hl + n * tile, tile), tile)
-            left = src[:, m].reshape(srows, part_d)
-            right = w[k, :, :, :, cols].reshape(part_d, tile)
-            got = jnp.dot(left, right, preferred_element_type=F32)
-            part[ph, :, streams[m], cols] = got.astype(BF).reshape(RING, mrows, tile)
+        cols = halves[half]
+        left = src[:, m].reshape(srows, part_d)
+        right = w[k, :, :, :, cols].reshape(part_d, hl)
+        got = jnp.dot(left, right, preferred_element_type=F32)
+        part[ph, :, streams[m], cols] = got.astype(BF).reshape(RING, mrows, hl)
 
     def widen(base, units_ref, k, out, m):
         for cc in range(2):
-            @pl.loop(0, 2)
-            def _(p):
-                cols = pl.ds(pl.multiple_of(cc * RING * sub + p * 2 * sub, tile), 2 * sub)
-                left = units_ref[:, streams[m], :].reshape(srows, hid)
-                right = w[k, cc, pl.ds(p * 2, 2)].reshape(2 * sub, hid)
-                add = lax.dot_general(left, right, NT, preferred_element_type=F32)
-                old = base[:, m, :, cols].reshape(srows, 2 * sub).astype(F32)
-                out[:, m, :, cols] = (old + add).astype(BF).reshape(RING, mrows, 2 * sub)
+            cols = pl.ds(cc * RING * sub, RING * sub)
+            left = units_ref[:, streams[m], :].reshape(srows, hid)
+            right = w[k, cc].reshape(RING * sub, hid)
+            add = lax.dot_general(left, right, NT, preferred_element_type=F32)
+            old = base[:, m, :, cols].reshape(srows, RING * sub).astype(F32)
+            out[:, m, :, cols] = (old + add).astype(BF).reshape(RING, mrows, RING * sub)
 
     def weight_grad(left_ref, right, k):
-        def side(cc, p):
-            zz = pl.ds(pl.multiple_of(p * 2, 2), 2)
-            cols = pl.ds(pl.multiple_of(cc * RING * sub + p * 2 * sub, tile), 2 * sub)
-            left = left_ref[:, :, :, cols].reshape(rows, 2 * sub)
+        def side(cc):
+            cols = pl.ds(pl.multiple_of(cc * RING * sub, tile), RING * sub)
+            left = left_ref[:, :, :, cols].reshape(rows, RING * sub)
             got = lax.dot_general(left, right[...].reshape(rows, hid), TN, preferred_element_type=F32)
-            g[k, cc, zz] = got.astype(BF).reshape(2, sub, hid)
+            g[k, cc] = got.astype(BF).reshape(RING, sub, hid)
 
         def across(p):
             zz = pl.ds(pl.multiple_of(p * 2, 2), 2)
@@ -229,12 +235,10 @@
 
         p_far = z2 // 2
         p_near = 1 - p_far
-        side(core2, p_far)
+        side(core2)
         far = across(p_far)
-        side(core2, p_near)
         near = across(p_near)
-        side(core, p_far)
-        side(core, p_near)
+        side(core)
         return q1(k, [far]), near
 
     def plus(x, *more):
@@ -255,6 +259,10 @@
 
     def slots(m):
         return pl.ds(m * crows, crows)
+
+    big = r1.at[:, pl.ds(0, 6)]
+    small = r2.at[:, :, pl.ds(0, 3)]
+    r1_out, r2_out, s1_out, s2_out = Outbox(big), Outbox(small), Outbox(small), Outbox(big)
 
     def r1_at(half, slot):
         return half * RING + slot
@@ -267,6 +275,7 @@
                 (part.at[ph, at, r, lanes], r1.at[ph, r1_at(half, slot), r], dev)
                 for slot, dev, at in first[half]
             ],
+            r1_out,
         )
 
     def rs2(ph, half, m, copies):
@@ -282,12 +291,14 @@
                 (part.at[ph, b, inner_rows(at, m), lanes], r2.at[ph, half, slot, slots(m)], dev)
                 for slot, dev, at in second[half]
             ],
+            r2_out,
         )
 
     def rs1_turned(ph, m):
         return group_of(
             rx.at[pl.ds(1, 3)],
             [(part.at[ph, :, inner_rows(at, m), halves[1]], rx.at[slot], dev) for slot, dev, at in xpeers],
+            r1_out,
         )
 
     def rs2_turned(ph, m, copies):
@@ -297,6 +308,7 @@
         return group_of(
             r2.at[ph, 1, pl.ds(1, 3), slots(m)],
             [(part.at[ph, at, mid, halves[1]], r2.at[ph, 1, slot, slots(m)], dev) for slot, dev, at in ypeers],
+            r2_out,
         )
 
     def units(ph, half, m, copies):
@@ -313,17 +325,19 @@
     def sp1(ref, half, m):
         piece = ref.at[block[half], inner_rows(inner[half], m), halves[half]]
         like = ref.at[block[half], pl.ds(m * mrows, 3 * crows), halves[half]]
-        return group_of(like, [(piece, piece, dev) for _, dev, _ in second[half]])
+        return group_of(like, [(piece, piece, dev) for _, dev, _ in second[half]], s1_out)
 
     def sp2(ref, half, m, copies):
         wait_all(copies)
         piece = ref.at[block[half], streams[m], halves[half]]
         like = ref.at[pl.ds(0, 3), streams[m], halves[half]]
-        return group_of(like, [(piece, piece, dev) for _, dev, _ in first[half]])
+        return group_of(like, [(piece, piece, dev) for _, dev, _ in first[half]], s2_out)
 
     def slope_of(upward, pre):
         sig = jax.nn.sigmoid(pre)
         return (upward * sig * (1.0 + pre * (1.0 - sig))).astype(BF)
+
+    q1_out, q2_out = Outbox(ra), Outbox(rb)
 
     def q1(k, copies):
         wait_all(copies)
@@ -334,6 +348,7 @@
                 (g.at[k, core, z2, lo, :], ra.at[k, 0], up),
                 (g.at[k, core, z2, hi, :], ra.at[k, 1], dn),
             ],
+            q1_out,
         )
 
     def q2(k, copies, near):
@@ -344,7 +359,9 @@
         g[k, core, zu, lo, :] = plus(g[k, core, zu, lo, :], rc[k, zu, lo, :], ra[k, 0]).astype(BF)
         g[k, core, zd, hi, :] = plus(g[k, core, zd, hi, :], rc[k, zd, hi, :], ra[k, 1]).astype(BF)
         return group_of(
-            rb.at[k], [(g.at[k, core, zu], rb.at[k, 0], up), (g.at[k, core, zd], rb.at[k, 1], dn)]
+            rb.at[k],
+            [(g.at[k, core, zu], rb.at[k, 0], up), (g.at[k, core, zd], rb.at[k, 1], dn)],
+            q2_out,
         )
 
     def fold(value):
@@ -458,10 +475,9 @@
     wait_all(cc3)
     wait_all(cd3)
     p20 = project_send(cot, 3, 2, 0)
+    p21 = project_send(cot, 3, 2, 1)
     wait_all(cb_own1)
     cd_own1 = g3(own1)
-    project(cot, 3, 2, 0, 1)
-    project(cot, 3, 2, 1, 1)
     wait_all(cb_got1)
     cd_got1 = g3(got1)
     settle(a00)
@@ -469,13 +485,12 @@
     wait_all(cd_own1 + cd_got1)
     widen(x0, act.at[0], 1, x1, 0)
     p10 = project_send(x1, 2, 1, 0)
-    p21 = both(lambda half: rs1(2, half, 1))
     settle(a01)
     widen(x0, act.at[0], 1, x1, 1)
     p11 = project_send(x1, 2, 1, 1)
     p20 = all_rs2(2, 0, p20)
+    p21 = all_rs2(2, 1, p21)
     p10 = all_rs2(1, 0, p10)
-    p21 = all_rs2(2, 1, p21)
     def open_slope(m, sent_up, sent_pre):
         done = []
         for half in HALVES:
@@ -497,11 +512,13 @@
     widen(cot, slope.at[1], 2, err1, 0)
     p30 = project_send(err1, 1, 3, 0)
     settle(s11)
-    d2, near2 = weight_grad(x1, slope.at[1], 2)
-    a10 = all_sp2(act.at[1], 0, a10)
     widen(cot, slope.at[1], 2, err1, 1)
     p31 = project_send(err1, 1, 3, 1)
+    a10 = all_sp2(act.at[1], 0, a10)
+    d2, near2 = weight_grad(x1, slope.at[1], 2)
     p30 = all_rs2(3, 0, p30)
+    p31 = all_rs2(3, 1, p31)
+    a11 = all_sp2(act.at[1], 1, a11)
     d1, near1 = weight_grad(err1, act.at[0], 1)
     d2 = q2(2, d2, near2)
     def close_slope(m, sent):
@@ -513,15 +530,13 @@
         return done
 
     s00 = close_slope(0, p30)
-    p31 = all_rs2(3, 1, p31)
-    a11 = all_sp2(act.at[1], 1, a11)
-    s00 = all_sp2(slope.at[0], 0, s00)
     s01 = close_slope(1, p31)
-    d1 = q2(1, d1, near1)
-    s01 = all_sp2(slope.at[0], 1, s01)
     settle(a10)
     settle(a11)
     d3, near3 = weight_grad(cot, act.at[1], 3)
+    s00 = all_sp2(slope.at[0], 0, s00)
+    s01 = all_sp2(slope.at[0], 1, s01)
+    d1 = q2(1, d1, near1)
     squares = finish(2, d2)
     settle(s00)
     settle(s01)
@@ -612,14 +627,14 @@
             pltpu.VMEM((8, 8, 128), F32),
             pltpu.VMEM((16, 8, 128), F32),
             pltpu.SemaphoreType.DMA((12,)),
-            pltpu.SemaphoreType.DMA((111,)),
+            pltpu.SemaphoreType.DMA((45,)),
             pltpu.SemaphoreType.DMA((111,)),
         ],
         compiler_params=pltpu.CompilerParams(
             collective_id=0, has_side_effects=True, vmem_limit_bytes=67043328
         ),
     )(inputs, w_in[0], w_out[0], cotangent)
-    steps = 4
+    steps = 2
     in_block = pl.BlockSpec((shard // steps, hid), lambda i: (i, 0))
     out_block = pl.BlockSpec((hid // steps, shard), lambda i: (i, 0))
     upd_in, upd_out = pl.pallas_call(

time: 140 us -> 134 us (0.957)
  Pallas kernels: 137 us -> 132 us
    pallas_call x1, Pallas kernels: 133 us -> 129 us  [on_device(): pl.pallas_call(kernel, out_shape=(jax.ShapeDtypeStruct((shard, hid), F32)...]
where the time goes in v7:
time: 134 us
  Pallas kernels  132 us (99%)
  between operations  2.39 us (2%)
    pallas_call x1, Pallas kernels, on_device(): pl.pallas_call(kernel, out_shape=(jax.ShapeDtypeStruct((shard, hid), F32)...  129 us
    pallas_call x1, Pallas kernels, on_device(): pl.pallas_call(clip, grid=(steps,), out_shape=(jax.ShapeDtypeStruct((shar...  3.25 us

profile of v7, /device:TPU:1, one launch (start us, length us, event | category | flops | bytes accessed | tf_op | source)
XLA Modules:
  0.0 134.3 jit_solution(5657174137704271561)
XLA Ops:
  0.6 128.7 %shard_map.67 = (f32[256,1024]{1,0:T(8,128)}, f32[1024,256]{1,0:T(8,128)}, f32[1,1]{1,0:T(1,128)}) custom-call(bf16[2,128,4096]{2,1,0:T(8,128)(2,1)} %x_hbm.1, bf16[256,1024]{1,0:T(8,128)(2,1)} %bitcast.5, bf16[1024,256]{1,0:T(8,128)(2,1)} %bitcast.6, bf16[2,128,4096]{2,1,0:T(8,128)(2,1)} %cot_hbm.1), custom_call_target="tpu_custom_call" | custom-call | tf_op jit(solution)/shard_map/pallas_call | solution.py:598
  129.3 3.3 %shard_map.68 = (f32[256,1024]{1,0:T(8,128)}, f32[1024,256]{1,0:T(8,128)}) custom-call(f32[1,1]{1,0:T(1,128)} %get-tuple-element.8.norm_ref, f32[256,1024]{1,0:T(8,128)} %get-tuple-element.9.tot_in, f32[1024,256]{1,0:T(8,128)} %get-tuple-element.10.tot_out), custom_call_target="tpu_custom_call" | custom-call | tf_op jit(solution)/shard_map/pallas_call | solution.py:640

commit v8 on v7

--- a/solution.py
+++ b/solution.py
@@ -239,7 +239,7 @@
         far = across(p_far)
         near = across(p_near)
         side(core)
-        return q1(k, [far]), near
+        return [far], near
 
     def plus(x, *more):
         total = x.astype(F32)
@@ -512,10 +512,11 @@
     widen(cot, slope.at[1], 2, err1, 0)
     p30 = project_send(err1, 1, 3, 0)
     settle(s11)
+    d2, near2 = weight_grad(x1, slope.at[1], 2)
     widen(cot, slope.at[1], 2, err1, 1)
     p31 = project_send(err1, 1, 3, 1)
+    d2 = q1(2, d2)
     a10 = all_sp2(act.at[1], 0, a10)
-    d2, near2 = weight_grad(x1, slope.at[1], 2)
     p30 = all_rs2(3, 0, p30)
     p31 = all_rs2(3, 1, p31)
     a11 = all_sp2(act.at[1], 1, a11)
@@ -530,17 +531,20 @@
         return done
 
     s00 = close_slope(0, p30)
+    d1 = q1(1, d1)
     s01 = close_slope(1, p31)
     settle(a10)
     settle(a11)
     d3, near3 = weight_grad(cot, act.at[1], 3)
     s00 = all_sp2(slope.at[0], 0, s00)
     s01 = all_sp2(slope.at[0], 1, s01)
+    d3 = q1(3, d3)
     d1 = q2(1, d1, near1)
     squares = finish(2, d2)
     settle(s00)
     settle(s01)
     d0, near0 = weight_grad(x0, slope.at[0], 0)
+    d0 = q1(0, d0)
     d3 = q2(3, d3, near3)
     squares = squares + finish(1, d1)
     d0 = q2(0, d0, near0)

time: 134 us -> 134 us (level)
  no operation moved by 1% of the time
where the time goes in v8:
time: 134 us
  Pallas kernels  131 us (98%)
  between operations  2.39 us (2%)
    pallas_call x1, Pallas kernels, on_device(): pl.pallas_call(kernel, out_shape=(jax.ShapeDtypeStruct((shard, hid), F32)...  128 us
    pallas_call x1, Pallas kernels, on_device(): pl.pallas_call(clip, grid=(steps,), out_shape=(jax.ShapeDtypeStruct((shar...  3.25 us

profile of v8, /device:TPU:1, one launch (start us, length us, event | category | flops | bytes accessed | tf_op | source)
XLA Modules:
  0.0 133.9 jit_solution(9538585713373768047)
XLA Ops:
  0.6 128.2 %shard_map.67 = (f32[256,1024]{1,0:T(8,128)}, f32[1024,256]{1,0:T(8,128)}, f32[1,1]{1,0:T(1,128)}) custom-call(bf16[2,128,4096]{2,1,0:T(8,128)(2,1)} %x_hbm.1, bf16[256,1024]{1,0:T(8,128)(2,1)} %bitcast.5, bf16[1024,256]{1,0:T(8,128)(2,1)} %bitcast.6, bf16[2,128,4096]{2,1,0:T(8,128)(2,1)} %cot_hbm.1), custom_call_target="tpu_custom_call" | custom-call | tf_op jit(solution)/shard_map/pallas_call | solution.py:602
  128.9 3.3 %shard_map.68 = (f32[256,1024]{1,0:T(8,128)}, f32[1024,256]{1,0:T(8,128)}) custom-call(f32[1,1]{1,0:T(1,128)} %get-tuple-element.8.norm_ref, f32[256,1024]{1,0:T(8,128)} %get-tuple-element.9.tot_in, f32[1024,256]{1,0:T(8,128)} %get-tuple-element.10.tot_out), custom_call_target="tpu_custom_call" | custom-call | tf_op jit(solution)/shard_map/pallas_call | solution.py:644
